TPU v7x, 32 devices: a whole 2x2x4 slice. The times are simulated.
32 devices in a mesh: enc: 8 (over z, x), tp: 4 (over y, core).
Axes of the slice: x: 2, y: 2, z: 4, core: 2. Of those that a mesh axis runs over, the one named last changes fastest.
Arguments:
- grad_rows: bfloat16 [3072, 8192], P('enc', 'tp'), may hold values from -6 to 6
- features: bfloat16 [3072, 1280], P('enc'), may hold values from -6 to 6
- block_in: bfloat16 [3072, 1280], P('enc', 'tp'), may hold values from -6 to 6
- patch_counts: int32 [8, 3], replicated, may hold values from 32 to 128, as said below
- owner: int32 [8, 3], replicated, may hold values from 0 to 7, as said below
- ln1_gain: float32 [1280], replicated, may hold values from 0.5 to 1.5
- w_qkv: bfloat16 [1280, 16, 240], P(None, 'tp')
- w_out: bfloat16 [1280, 1280], P('tp'), may hold values from -0.15625 to 0.15625
- w_proj: bfloat16 [1280, 8192], P(None, 'tp'), may hold values from -0.15625 to 0.15625
Outputs:
- grad_input: bfloat16 [3072, 1280], P('enc', 'tp')
- grad_proj: float32 [1280, 8192], P('enc', 'tp')
- grad_qkv: float32 [1280, 16, 240], P('enc', 'tp')
- grad_out: float32 [1280, 1280], P('tp', 'enc')
- grad_ln1: float32 [1280], P('enc')
Inputs may be any that keep to these rules, and one draw needn't show every extreme that they name: `patch_counts`: some image has exactly 128 live rows and some exactly 32. `owner`: each encoder device receives exactly 3 images, never two from the same block.
All inputs are finite; a program needn't handle non-finite values.
Results may differ from a plain program's by a relative error of at most 0.033.
Values may be sent and summed in bfloat16 or wider, within the bound.
A program may use at most 64 MiB of HBM per device.

v0:
```python
import jax
import jax.numpy as jnp
from jax import lax
from jax.experimental import pallas as pl
from jax.experimental.pallas import tpu as pltpu
from jax.sharding import PartitionSpec as P


TILE = 128


EPSILON = 1e-05


def dot_nt(left, right):
    return lax.dot_general(
        left, right, (((1,), (1,)), ((), ())), preferred_element_type=jnp.float32
    )


def dot_tn(left, right):
    return lax.dot_general(
        left, right, (((0,), (0,)), ((), ())), preferred_element_type=jnp.float32
    )


def inner_size(groups):
    inner = 1
    while inner * inner * 4 <= groups:
        inner *= 2
    return inner


def pick(values, place, dim):
    return lax.dynamic_index_in_dim(values, place, dim, keepdims=False, allow_negative_indices=False)


def two_stage_sum(left, right, axis, inner, whole=False):
    total = left.shape[0]
    outer = total // inner
    index = lax.axis_index(axis).astype(jnp.uint32)
    at_outer, at_inner = lax.div(index, jnp.uint32(inner)), lax.rem(index, jnp.uint32(inner))
    lefts = left.reshape((outer, inner) + left.shape[1:])

    if whole:
        every = jnp.dot(left.reshape(-1, left.shape[2]), right, preferred_element_type=jnp.float32)
        every = every.astype(jnp.bfloat16).reshape((outer, inner) + (left.shape[1], right.shape[1]))

    def term(place):
        if whole:
            return pick(every, place, 1)
        chosen = pick(lefts, place, 1)
        flat = chosen.reshape(-1, chosen.shape[-1])
        product = jnp.dot(flat, right, preferred_element_type=jnp.float32).astype(jnp.bfloat16)
        return product.reshape(outer, -1, right.shape[1])

    arrived = []
    for step in range(1, inner):
        pairs = [(o * inner + i, o * inner + (i + step) % inner) for o in range(outer) for i in range(inner)]
        sent = term(lax.rem(at_inner + jnp.uint32(step), jnp.uint32(inner)))
        arrived.append(lax.ppermute(sent, axis, pairs))
    running = term(at_inner).astype(jnp.float32)
    for value in arrived:
        running += value.astype(jnp.float32)
    summed = pick(running, at_outer, 0)
    short = running.astype(jnp.bfloat16)
    arrived = []
    for step in range(1, outer):
        pairs = [(o * inner + i, (o + step) % outer * inner + i) for o in range(outer) for i in range(inner)]
        sent = pick(short, lax.rem(at_outer + jnp.uint32(step), jnp.uint32(outer)), 0)
        arrived.append(lax.ppermute(sent, axis, pairs))
    for value in arrived:
        summed += value.astype(jnp.float32)
    return summed


def summed_rows(left, right, axis, inner, cuts):
    rows = left.shape[1]
    if rows % (16 * cuts):
        cuts = 1
    height = rows // cuts
    pieces = [two_stage_sum(left[:, c * height : (c + 1) * height], right, axis, inner) for c in range(cuts)]
    return jnp.concatenate(pieces, axis=0) if cuts > 1 else pieces[0]


def small_sum(part, axis):
    total = part.shape[0]
    index = lax.axis_index(axis).astype(jnp.uint32)
    summed = pick(part, index, 0).astype(jnp.float32)
    for step in range(1, total):
        pairs = [(i, (i + step) % total) for i in range(total)]
        sent = pick(part, lax.rem(index + jnp.uint32(step), jnp.uint32(total)), 0)
        summed += lax.ppermute(sent, axis, pairs).astype(jnp.float32)
    return summed


def attend_kernel(size, counts_ref, packed_ref, prob_ref, mixed_ref):
    tile = packed_ref.shape[0]
    count = counts_ref[pl.program_id(0)]
    rows = lax.broadcasted_iota(jnp.int32, (tile, tile), 0) < count
    columns = lax.broadcasted_iota(jnp.int32, (tile, tile), 1) < count
    same = jnp.logical_not(jnp.logical_xor(rows, columns))
    scaling = 1.0 / size**0.5
    for h in range(prob_ref.shape[1]):
        base = h * 3 * size
        queries = packed_ref[:, base : base + size]
        keys = packed_ref[:, base + size : base + 2 * size]
        values = packed_ref[:, base + 2 * size : base + 3 * size]
        scores = jnp.where(same, dot_nt(queries, keys) * scaling, -1e30)
        terms = jnp.exp(scores - jnp.max(scores, axis=-1, keepdims=True))
        probability = terms / jnp.sum(terms, axis=-1, keepdims=True)
        prob_ref[0, h] = probability
        mixed = jnp.dot(probability.astype(jnp.bfloat16), values, preferred_element_type=jnp.float32)
        mixed_ref[:, h * size : (h + 1) * size] = mixed.astype(jnp.bfloat16)


def attend(packed, counts, heads, size):
    rows = packed.shape[0]
    images = rows // TILE
    return pl.pallas_call(
        lambda *refs: attend_kernel(size, *refs),
        grid=(images,),
        in_specs=[
            pl.BlockSpec(memory_space=pltpu.SMEM),
            pl.BlockSpec((TILE, packed.shape[1]), lambda i: (i, 0)),
        ],
        out_specs=[
            pl.BlockSpec((1, heads, TILE, TILE), lambda i: (i, 0, 0, 0)),
            pl.BlockSpec((TILE, heads * size), lambda i: (i, 0)),
        ],
        out_shape=[
            jax.ShapeDtypeStruct((images, heads, TILE, TILE), jnp.float32),
            jax.ShapeDtypeStruct((rows, heads * size), jnp.bfloat16),
        ],
        cost_estimate=pl.CostEstimate(flops=2 * 10**9, bytes_accessed=4 * 10**6, transcendentals=0),
        name="attend",
    )(counts, packed)


def attend_back_kernel(size, packed_ref, prob_ref, vis_ref, out_ref, grad_ref):
    scaling = 1.0 / size**0.5
    mixed_grads = lax.dot_general(
        vis_ref[...], out_ref[...], (((0,), (1,)), ((), ())), preferred_element_type=jnp.float32
    ).astype(jnp.bfloat16)
    for h in range(prob_ref.shape[1]):
        base = h * 3 * size
        queries = packed_ref[:, base : base + size]
        keys = packed_ref[:, base + size : base + 2 * size]
        values = packed_ref[:, base + 2 * size : base + 3 * size]
        mixed_grad = mixed_grads[:, h * size : (h + 1) * size]
        probability = prob_ref[0, h]
        prob_grad = dot_nt(mixed_grad, values)
        inner = jnp.sum(probability * prob_grad, axis=-1, keepdims=True)
        score_grad = (probability * (prob_grad - inner) * scaling).astype(jnp.bfloat16)
        prob_low = probability.astype(jnp.bfloat16)
        q_grad = jnp.dot(score_grad, keys, preferred_element_type=jnp.float32)
        grad_ref[:, base : base + size] = q_grad.astype(jnp.bfloat16)
        grad_ref[:, base + size : base + 2 * size] = dot_tn(score_grad, queries).astype(jnp.bfloat16)
        grad_ref[:, base + 2 * size : base + 3 * size] = dot_tn(prob_low, mixed_grad).astype(jnp.bfloat16)


def attend_back(packed, probability, vis_low, w_out, size):
    rows, width = packed.shape
    images, heads = probability.shape[:2]
    return pl.pallas_call(
        lambda *refs: attend_back_kernel(size, *refs),
        grid=(images,),
        in_specs=[
            pl.BlockSpec((TILE, width), lambda i: (i, 0)),
            pl.BlockSpec((1, heads, TILE, TILE), lambda i: (i, 0, 0, 0)),
            pl.BlockSpec((vis_low.shape[0], TILE), lambda i: (0, i)),
            pl.BlockSpec(w_out.shape, lambda i: (0, 0)),
        ],
        out_specs=pl.BlockSpec((TILE, width), lambda i: (i, 0)),
        out_shape=jax.ShapeDtypeStruct((rows, width), jnp.bfloat16),
        cost_estimate=pl.CostEstimate(flops=3 * 10**9, bytes_accessed=6 * 10**6, transcendentals=0),
        name="attend_back",
    )(packed, probability, vis_low, w_out)


def gathered(share, axis):
    total = lax.axis_size(axis)
    index = lax.axis_index(axis).astype(jnp.uint32)
    stacked = [share]
    for step in range(1, total):
        pairs = [(i, (i - step) % total) for i in range(total)]
        stacked.append(lax.ppermute(share, axis, pairs))
    twice = jnp.concatenate([part[None] for part in stacked + stacked[:-1]], axis=0)
    return lax.dynamic_slice_in_dim(twice, lax.rem(jnp.uint32(total) - index, jnp.uint32(total)), total, 0) if total > 1 else twice


def shards(grad_rows, features, block_in, patch_counts, owner, ln1_gain, w_qkv, w_out, w_proj):
    groups = lax.axis_size("enc")
    tp_size = lax.axis_size("tp")
    inner = inner_size(groups)
    device = lax.axis_index("enc")
    tp_rank = lax.axis_index("tp")
    block_rows = grad_rows.shape[0]
    img_group = block_rows // TILE
    share_width = block_in.shape[1]
    features_dim = features.shape[1]
    line_index = jnp.arange(TILE, dtype=jnp.int32)
    peer_index = jnp.arange(groups, dtype=jnp.int32)
    own_counts = lax.dynamic_index_in_dim(patch_counts, device, 0, keepdims=False)
    own_owner = lax.dynamic_index_in_dim(owner, device, 0, keepdims=False)
    live_own = line_index[None, :] < own_counts[:, None]

    sends = jnp.any(owner == device, axis=1)
    sends_int = sends.astype(jnp.int32)
    rank = jnp.cumsum(sends_int) - sends_int
    slot_index = jnp.arange(img_group, dtype=jnp.int32)
    source_of = jnp.sum(
        jnp.where(sends[None, :] & (rank[None, :] == slot_index[:, None]), peer_index[None, :], 0),
        axis=1,
    )
    source_owner = jnp.take(owner, source_of, axis=0)
    source_counts = jnp.take(patch_counts, source_of, axis=0)
    arrived_counts = jnp.sum(jnp.where(source_owner == device, source_counts, 0), axis=1)

    kept_rows = jnp.where(live_own.reshape(-1)[:, None], features, jnp.zeros_like(features))
    piece_rows = features_dim // groups
    grad_proj = summed_rows(kept_rows.T.reshape(groups, piece_rows, block_rows), grad_rows, "enc", inner, 2)

    shared = two_stage_sum(w_proj.reshape(tp_size, share_width, w_proj.shape[1]), grad_rows.T, "tp", 2, whole=True)
    tiles = jnp.where(live_own.reshape(-1)[None, :], shared, 0.0).astype(jnp.bfloat16)
    tiles = [tiles[:, j * TILE : (j + 1) * TILE] for j in range(img_group)]
    outgoing = jnp.zeros((groups, share_width, TILE), jnp.bfloat16)
    for j in range(img_group):
        outgoing = jnp.where((own_owner[j] == peer_index)[:, None, None], tiles[j][None], outgoing)
    received = lax.all_to_all(outgoing, "enc", split_axis=0, concat_axis=0, tiled=True)
    vis_share = jnp.concatenate([pick(received, source_of[j].astype(jnp.uint32), 0) for j in range(img_group)], axis=1)
    vis_low = gathered(vis_share, "tp").reshape(features_dim, block_rows)

    heads_here = w_qkv.shape[1]
    head_size = w_qkv.shape[2] // 3
    block_turned = block_in.T
    block_full = gathered(block_turned, "tp").reshape(features_dim, block_rows)
    qkv_flat = w_qkv.reshape(features_dim, heads_here * 3 * head_size)
    block_wide = block_full.astype(jnp.float32)
    centre = jnp.mean(block_wide, axis=0, keepdims=True)
    centred = block_wide - centre
    inverse1 = lax.rsqrt(jnp.mean(centred * centred, axis=0, keepdims=True) + EPSILON)
    normed_in = (centred * inverse1 * ln1_gain[:, None]).astype(jnp.bfloat16)
    packed = dot_tn(normed_in, qkv_flat).astype(jnp.bfloat16)
    probability, mixed = attend(packed, arrived_counts, heads_here, head_size)
    packed_grad = attend_back(packed, probability, vis_low, w_out, head_size)

    in_sum = two_stage_sum(
        qkv_flat.reshape(tp_size, share_width, qkv_flat.shape[1]), packed_grad.T, "tp", 2, whole=True
    )
    normed_share = (block_turned.astype(jnp.float32) - centre) * inverse1
    gain_share = lax.dynamic_slice_in_dim(ln1_gain, tp_rank * share_width, share_width, 0)
    scaled = in_sum * gain_share[:, None]
    sums = jnp.concatenate([jnp.sum(scaled, axis=0), jnp.sum(scaled * normed_share, axis=0)])
    ln1_share = jnp.sum(in_sum * normed_share, axis=1)
    small = jnp.concatenate([sums, ln1_share])
    small = gathered(small, "tp")
    means = jnp.sum(small[:, : 2 * block_rows], axis=0).reshape(2, 1, block_rows) / features_dim
    in_back = inverse1 * (scaled - means[0] - normed_share * means[1])
    grad_input = (vis_share.astype(jnp.float32) + in_back).astype(jnp.bfloat16).T

    grad_qkv = summed_rows(
        normed_in.reshape(groups, piece_rows, block_rows), packed_grad, "enc", inner, 2
    ).reshape(piece_rows, heads_here, 3 * head_size)
    grad_out = two_stage_sum(vis_low.reshape(groups, piece_rows, block_rows), mixed, "enc", inner).T
    ln1_term = small[:, 2 * block_rows :].reshape(groups, piece_rows).astype(jnp.bfloat16)
    grad_ln1 = small_sum(ln1_term, "enc")
    return (grad_input, grad_proj, grad_qkv, grad_out, grad_ln1)


def solution(mesh):
    placed = (
        P("enc", "tp"),
        P("enc", None),
        P("enc", "tp"),
        P(),
        P(),
        P(),
        P(None, "tp", None),
        P("tp", None),
        P(None, "tp"),
    )
    return jax.shard_map(
        shards,
        mesh=mesh,
        in_specs=placed,
        out_specs=(P("enc", "tp"), P("enc", "tp"), P("enc", "tp", None), P("tp", "enc"), P("enc")),
        check_vma=False,
    )
```

profile of v0, /device:TPU:0, one launch (start us, length us, event | category | flops | bytes accessed | tf_op | source)
XLA Modules:
  0.0 262.9 jit_solution(1302296332967284393)
XLA Ops:
  0.6 2.5 collective-permute-start.2
  3.9 5.9 %convolution_convert_fusion.1 = bf16[1280,384]{1,0:T(8,128)(2,1)S(1)} fusion(bf16[1280,2048]{1,0:T(8,128)(2,1)} %param.19, bf16[384,2048]{1,0:T(8,128)(2,1)} %param.11), kind=kOutput, calls=%fused_computation.3 | convolution fusion | flops 2013757440 | bytes 7798784 | tf_op jit(solution)/shard_map/dot_general | solution.py:46
  11.7 1.4 collective-permute-start
  13.3 1.6 copy.38
  16.4 1.9 convolution_convert_fusion.4
  18.3 1.5 collective-permute-start.13
  22.1 3.5 %convolution_convert_fusion.5 = bf16[320,2048]{1,0:T(8,128)(2,1)} fusion(bf16[320,384]{1,0:T(8,128)(2,1)S(1)} %bitcast.241, bf16[384,2048]{1,0:T(8,128)(2,1)} %param.11), kind=kOutput, calls=%fused_computation.7 | convolution fusion | flops 503971840 | bytes 3129344 | tf_op jit(solution)/shard_map/dot_general | solution.py:54
  25.6 1.9 convolution_convert_fusion.2
  27.5 1.9 convolution_convert_fusion.3
  36.1 1.7 bitcast_dynamic-update-slice_fusion.12
  37.7 1.7 bitcast_dynamic-update-slice_fusion.10
  39.4 1.7 bitcast_dynamic-update-slice_fusion.9
  41.8 1.7 bitcast_dynamic-update-slice_fusion.13
  43.5 1.7 bitcast_dynamic-update-slice_fusion.11
  45.2 1.4 convert_reduce_fusion
  46.6 1.5 dynamic-slice_convert_fusion
  49.5 2.1 convolution_convert_fusion.6.refs_1_.refs_0_
  55.1 6.6 %attend.1 = (f32[3,4,128,128]{3,2,1,0:T(8,128)}, bf16[384,320]{1,0:T(8,128)(2,1)}) custom-call(s32[3]{0:T(128)} %fusion.19.refs_0_, bf16[384,960]{1,0:T(8,128)(2,1)} %convolution_convert_fusion.6.refs_1_.refs_0_), custom_call_target="tpu_custom_call" | custom-call | flops 2000000000 | bytes 4000000 | tf_op jit(solution)/shard_map/attend/pallas_call | solution.py:120
  63.9 5.8 %all-to-all-start = ((bf16[8,320,128]{2,1,0:T(8,128)(2,1)}), bf16[8,320,128]{2,1,0:T(8,128)(2,1)}, u32[]{:S(2)}, u32[]{:S(2)}) async-start(bf16[8,320,128]{2,1,0:T(8,128)(2,1)} %select_select_fusion), calls=%async_computation | async-start | bytes 1310720 | tf_op jit(solution)/shard_map/all_to_all | solution.py:230
  69.7 2.3 convert_add_fusion.1
  72.1 2.3 collective-permute-start.14
  74.3 2.4 collective-permute-start.15
  76.7 1.5 collective-permute-start.16
  78.1 4.5 %collective-permute-done.17 = bf16[4,80,2048]{2,1,0:T(8,128)(2,1)} collective-permute-done((bf16[4,80,2048]{2,1,0:T(8,128)(2,1)}, bf16[4,80,2048]{2,1,0:T(8,128)(2,1)}, u32[]{:S(2)}, u32[]{:S(2)}) %collective-permute-start.17) | collective-permute-done | bytes 1310752 | tf_op jit(solution)/shard_map/ppermute | solution.py:61
  82.7 1.9 convert_add_fusion
  84.6 1.6 collective-permute-start.18
  86.2 3.5 %collective-permute-start.19 = (bf16[80,2048]{1,0:T(8,128)(2,1)S(1)}, bf16[80,2048]{1,0:T(8,128)(2,1)S(1)}, u32[]{:S(2)}, u32[]{:S(2)}) collective-permute-start(bf16[80,2048]{1,0:T(8,128)(2,1)S(1)} %get-tuple-element.35), channel_id=1, source_target_pairs={{0,16},{4,20},{8,24},{12,28},{16,0},{20,4},{24,8},{28,12},{1,17},{... | collective-permute-start | bytes 983048 | tf_op jit(solution)/shard_map/ppermute | solution.py:71
  89.7 3.1 %collective-permute-done.14 = bf16[80,2048]{1,0:T(8,128)(2,1)S(1)} collective-permute-done((bf16[80,2048]{1,0:T(8,128)(2,1)S(1)}, bf16[80,2048]{1,0:T(8,128)(2,1)S(1)}, u32[]{:S(2)}, u32[]{:S(2)}) %collective-permute-start.14) | collective-permute-done | bytes 327712 | tf_op jit(solution)/shard_map/ppermute | solution.py:71
  92.8 30.5 %collective-permute-done.15 = bf16[80,2048]{1,0:T(8,128)(2,1)S(1)} collective-permute-done((bf16[80,2048]{1,0:T(8,128)(2,1)S(1)}, bf16[80,2048]{1,0:T(8,128)(2,1)S(1)}, u32[]{:S(2)}, u32[]{:S(2)}) %collective-permute-start.15) | collective-permute-done | bytes 327712 | tf_op jit(solution)/shard_map/ppermute | solution.py:71
  123.5 13.9 %collective-permute-done.19 = bf16[80,2048]{1,0:T(8,128)(2,1)S(1)} collective-permute-done((bf16[80,2048]{1,0:T(8,128)(2,1)S(1)}, bf16[80,2048]{1,0:T(8,128)(2,1)S(1)}, u32[]{:S(2)}, u32[]{:S(2)}) %collective-permute-start.19) | collective-permute-done | bytes 327712 | tf_op jit(solution)/shard_map/ppermute | solution.py:71
  139.5 2.3 pad_maximum_fusion
  141.8 1.4 collective-permute-start.6
  143.5 7.1 %collective-permute-done.6 = bf16[320,384]{1,0:T(8,128)(2,1)S(1)} collective-permute-done((bf16[320,384]{1,0:T(8,128)(2,1)S(1)}, bf16[320,384]{1,0:T(8,128)(2,1)S(1)}, u32[]{:S(2)}, u32[]{:S(2)}) %collective-permute-start.6) | collective-permute-done | bytes 245792 | tf_op jit(solution)/shard_map/ppermute | solution.py:187
  150.6 2.3 collective-permute-done.7
  154.2 8.1 %attend_back.1 = bf16[384,960]{1,0:T(8,128)(2,1)} custom-call(bf16[384,960]{1,0:T(8,128)(2,1)} %convolution_convert_fusion.6.refs_1_.refs_0_, f32[3,4,128,128]{3,2,1,0:T(8,128)} %get-tuple-element.8.refs_1_, bf16[1280,384]{1,0:T(8,128)(2,1)} %bitcast.221, bf16[320,1280]{1,0:T(8,128)(2,1)} %refs_3_.1), custom_call_target="tpu_custom_call" | custom-call | flops 3000000000 | bytes 6000000 | tf_op jit(solution)/shard_map/attend_back/pallas_call | solution.py:165
  162.3 3.3 %fusion = bf16[1280,384]{0,1:T(8,128)(2,1)} fusion(bf16[384,960]{1,0:T(8,128)(2,1)} %attend_back.1, bf16[1280,960]{0,1:T(8,128)(2,1)S(1)} %bitcast.217), kind=kOutput, calls=%fused_computation.10 | convolution fusion | flops 944209920 | bytes 4177920 | tf_op jit(solution)/shard_map/dot_general | solution.py:46
  165.6 1.6 copy.37
  168.3 2.1 constant_dynamic-slice_fusion.9
  171.6 2.0 copy.44
  174.4 2.3 convolution_convert_fusion.9
  178.0 1.4 convolution_convert_fusion.10
  179.3 1.4 convolution_convert_fusion.7
  182.8 1.4 fusion.1
  184.2 1.5 copy.43
  185.7 2.4 collective-permute-done.29
  189.4 5.8 %collective-permute-start.30 = (bf16[160,320]{1,0:T(8,128)(2,1)S(1)}, bf16[160,320]{1,0:T(8,128)(2,1)S(1)}, u32[]{:S(2)}, u32[]{:S(2)}) collective-permute-start(bf16[160,320]{1,0:T(8,128)(2,1)S(1)} %get-tuple-element.51), channel_id=1, source_target_pairs={{0,8},{4,12},{8,16},{12,20},{16,24},{20,28},{24,0},{28,4},{1,9},{5... | collective-permute-start | bytes 307208 | tf_op jit(solution)/shard_map/ppermute | solution.py:71
  201.1 2.5 collective-permute-done.31
  204.6 2.5 convert_add_fusion.3
  207.9 3.2 %collective-permute-start.22 = (bf16[80,960]{1,0:T(8,128)(2,1)}, bf16[80,960]{1,0:T(8,128)(2,1)}, u32[]{:S(2)}, u32[]{:S(2)}) collective-permute-start(bf16[80,960]{1,0:T(8,128)(2,1)} %get-tuple-element.42), channel_id=1, source_target_pairs={{0,8},{4,12},{8,16},{12,20},{16,24},{20,28},{24,0},{28,4},{1,9},{5... | collective-permute-start | bytes 460808 | tf_op jit(solution)/shard_map/ppermute | solution.py:71
  212.2 3.2 %collective-permute-done.25 = bf16[4,80,960]{2,1,0:T(8,128)(2,1)} collective-permute-done((bf16[4,80,960]{2,1,0:T(8,128)(2,1)}, bf16[4,80,960]{2,1,0:T(8,128)(2,1)}, u32[]{:S(2)}, u32[]{:S(2)}) %collective-permute-start.25) | collective-permute-done | bytes 614432 | tf_op jit(solution)/shard_map/ppermute | solution.py:61
  215.4 2.4 convert_add_fusion.2
  220.5 1.6 collective-permute-done.11
  227.0 6.4 %collective-permute-start.34 = (bf16[160]{0:T(256)(128)(2,1)S(1)}, bf16[160]{0:T(256)(128)(2,1)S(1)}, u32[]{:S(2)}, u32[]{:S(2)}) collective-permute-start(bf16[160]{0:T(256)(128)(2,1)S(1)} %get-tuple-element.19), channel_id=1, source_target_pairs={{0,8},{4,12},{8,16},{12,20},{16,24},{20,28},{24,0},{28,4},{1,9},{5... | collective-permute-start | bytes 968 | tf_op jit(solution)/shard_map/ppermute | solution.py:93
  233.4 1.5 collective-permute-start.35
  234.9 2.1 fusion.12
  237.0 2.4 collective-permute-start.36
  239.3 1.7 collective-permute-start.37
  241.7 1.5 collective-permute-start.39
  243.8 2.1 collective-permute-start.24
  246.0 1.7 collective-permute-start.27
  248.2 2.1 collective-permute-start.28
  250.4 4.7 %collective-permute-done.24 = bf16[80,960]{1,0:T(8,128)(2,1)S(1)} collective-permute-done((bf16[80,960]{1,0:T(8,128)(2,1)}, bf16[80,960]{1,0:T(8,128)(2,1)S(1)}, u32[]{:S(2)}, u32[]{:S(2)}) %collective-permute-start.24) | collective-permute-done | bytes 153632 | tf_op jit(solution)/shard_map/ppermute | solution.py:71
  256.3 4.1 %collective-permute-done.27 = bf16[80,960]{1,0:T(8,128)(2,1)S(1)} collective-permute-done((bf16[80,960]{1,0:T(8,128)(2,1)}, bf16[80,960]{1,0:T(8,128)(2,1)S(1)}, u32[]{:S(2)}, u32[]{:S(2)}) %collective-permute-start.27) | collective-permute-done | bytes 153632 | tf_op jit(solution)/shard_map/ppermute | solution.py:71
  261.5 1.4 reshape.306
  (186 shorter events, 51.4 us)
Async XLA Ops:
  0.6 48.8 %copy-start = (bf16[1280,4,240]{0,2,1:T(8,128)(2,1)S(1)}, bf16[1280,4,240]{0,2,1:T(8,128)(2,1)}, u32[]{:S(2)}) copy-start(bf16[1280,4,240]{0,2,1:T(8,128)(2,1)} %param.17) | copy-start | bytes 7372804
  0.6 34.9 %collective-permute-start.2 = (bf16[320,384]{1,0:T(8,128)(2,1)}, bf16[320,384]{1,0:T(8,128)(2,1)}, u32[]{:S(2)}, u32[]{:S(2)}) collective-permute-start(bf16[320,384]{1,0:T(8,128)(2,1)} %bitcast.227), channel_id=1, source_target_pairs={{0,3},{1,0},{2,1},{3,2},{4,7},{5,4},{6,5},{7,6},{8,11},{9,8},{10,9... | collective-permute-start | bytes 737288 | tf_op jit(solution)/shard_map/ppermute | solution.py:187
  3.1 34.6 %collective-permute-start.3 = (bf16[320,384]{1,0:T(8,128)(2,1)}, bf16[320,384]{1,0:T(8,128)(2,1)}, u32[]{:S(2)}, u32[]{:S(2)}) collective-permute-start(bf16[320,384]{1,0:T(8,128)(2,1)} %bitcast.228), channel_id=1, source_target_pairs={{0,2},{1,3},{2,0},{3,1},{4,6},{5,7},{6,4},{7,5},{8,10},{9,11},{10,... | collective-permute-start | bytes 737288 | tf_op jit(solution)/shard_map/ppermute | solution.py:187
  3.8 35.6 %collective-permute-start.4 = (bf16[320,384]{1,0:T(8,128)(2,1)}, bf16[320,384]{1,0:T(8,128)(2,1)}, u32[]{:S(2)}, u32[]{:S(2)}) collective-permute-start(bf16[320,384]{1,0:T(8,128)(2,1)} %bitcast.229), channel_id=1, source_target_pairs={{0,1},{1,2},{2,3},{3,0},{4,5},{5,6},{6,7},{7,4},{8,9},{9,10},{10,1... | collective-permute-start | bytes 737288 | tf_op jit(solution)/shard_map/ppermute | solution.py:187
  3.9 9.1 %copy-start.26 = (s32[8,3]{0,1:T(4,128)S(1)}, s32[8,3]{0,1:T(4,128)}, u32[]{:S(2)}) copy-start(s32[8,3]{0,1:T(4,128)} %param.14) | copy-start | bytes 292
  11.7 39.9 %collective-permute-start = (bf16[2,320,384]{2,1,0:T(8,128)(2,1)}, bf16[2,320,384]{2,1,0:T(8,128)(2,1)}, u32[]{:S(2)}, u32[]{:S(2)}) collective-permute-start(bf16[2,320,384]{2,1,0:T(8,128)(2,1)} %dynamic-slice_bitcast_fusion.1), channel_id=1, source_target_pairs={{0,1},{1,0},{2,3},{3,2},{4,5},{5,4},{6,7},{7,6},{8,9},{9,8},{10,11... | collective-permute-start | bytes 1474568 | tf_op jit(solution)/shard_map/ppermute | solution.py:61
  16.4 3.4 %copy-start.25 = (s32[8,3]{0,1:T(4,128)S(1)}, s32[8,3]{0,1:T(4,128)}, u32[]{:S(2)}) copy-start(s32[8,3]{0,1:T(4,128)} %param.15) | copy-start | bytes 292
  16.4 3.5 %copy-start.8 = (bf16[384,320]{0,1:T(8,128)(2,1)S(1)}, bf16[384,320]{0,1:T(8,128)(2,1)}, u32[]{:S(2)}) copy-start(bf16[384,320]{0,1:T(8,128)(2,1)} %param.13) | copy-start | bytes 737284
  18.3 51.3 %collective-permute-start.13 = (bf16[4,80,2048]{2,1,0:T(8,128)(2,1)}, bf16[4,80,2048]{2,1,0:T(8,128)(2,1)}, u32[]{:S(2)}, u32[]{:S(2)}) collective-permute-start(bf16[4,80,2048]{2,1,0:T(8,128)(2,1)} %bitcast.42), channel_id=1, source_target_pairs={{0,4},{4,0},{8,12},{12,8},{16,20},{20,16},{24,28},{28,24},{1,5},{5... | collective-permute-start | bytes 3932168 | tf_op jit(solution)/shard_map/ppermute | solution.py:61
  22.1 3.5 %copy-start.2 = (bf16[384,2048]{1,0:T(8,128)(2,1)S(1)}, bf16[384,2048]{1,0:T(8,128)(2,1)}, u32[]{:S(2)}) copy-start(bf16[384,2048]{1,0:T(8,128)(2,1)} %param.11) | copy-start | bytes 4718596
  27.5 5.9 %copy-start.23 = (f32[1280]{0:T(1024)S(1)}, f32[1280]{0:T(1024)}, u32[]{:S(2)}) copy-start(f32[1280]{0:T(1024)} %param.16) | copy-start | bytes 15364
  35.5 182.4 %copy-start.24 = (f32[320]{0:T(512)}, f32[320]{0:T(512)S(1)}, u32[]{:S(2)}) copy-start(f32[320]{0:T(512)S(1)} %dynamic_slice.194) | copy-start | bytes 3844
  35.5 47.2 %collective-permute-start.17 = (bf16[4,80,2048]{2,1,0:T(8,128)(2,1)}, bf16[4,80,2048]{2,1,0:T(8,128)(2,1)}, u32[]{:S(2)}, u32[]{:S(2)}) collective-permute-start(bf16[4,80,2048]{2,1,0:T(8,128)(2,1)} %bitcast.230), channel_id=1, source_target_pairs={{0,4},{4,0},{8,12},{12,8},{16,20},{20,16},{24,28},{28,24},{1,5},{5... | collective-permute-start | bytes 3932168 | tf_op jit(solution)/shard_map/ppermute | solution.py:61
  49.5 2.1 copy-start.21
  53.5 8.2 %collective-permute-start.1 = (bf16[320,384]{1,0:T(8,128)(2,1)}, bf16[320,384]{1,0:T(8,128)(2,1)}, u32[]{:S(2)}, u32[]{:S(2)}) collective-permute-start(bf16[320,384]{1,0:T(8,128)(2,1)} %fusion.13), channel_id=1, source_target_pairs={{0,2},{1,3},{2,0},{3,1},{4,6},{5,7},{6,4},{7,5},{8,10},{9,11},{10,... | collective-permute-start | bytes 737288 | tf_op jit(solution)/shard_map/ppermute | solution.py:71
  63.9 74.5 %all-to-all-start = ((bf16[8,320,128]{2,1,0:T(8,128)(2,1)}), bf16[8,320,128]{2,1,0:T(8,128)(2,1)}, u32[]{:S(2)}, u32[]{:S(2)}) async-start(bf16[8,320,128]{2,1,0:T(8,128)(2,1)} %select_select_fusion), calls=%async_computation | async-start | bytes 1310720 | tf_op jit(solution)/shard_map/all_to_all | solution.py:230
  72.0 10.7 %copy-start.5 = (bf16[320,2048]{1,0:T(8,128)(2,1)S(1)}, bf16[320,2048]{1,0:T(8,128)(2,1)}, u32[]{:S(2)}) copy-start(bf16[320,2048]{1,0:T(8,128)(2,1)} %convolution_convert_fusion.3) | copy-start | bytes 3932164
  72.1 20.8 %collective-permute-start.14 = (bf16[80,2048]{1,0:T(8,128)(2,1)S(1)}, bf16[80,2048]{1,0:T(8,128)(2,1)S(1)}, u32[]{:S(2)}, u32[]{:S(2)}) collective-permute-start(bf16[80,2048]{1,0:T(8,128)(2,1)S(1)} %get-tuple-element.30), channel_id=1, source_target_pairs={{0,8},{4,12},{8,16},{12,20},{16,24},{20,28},{24,0},{28,4},{1,9},{5... | collective-permute-start | bytes 983048 | tf_op jit(solution)/shard_map/ppermute | solution.py:71
  74.3 49.0 %collective-permute-start.15 = (bf16[80,2048]{1,0:T(8,128)(2,1)S(1)}, bf16[80,2048]{1,0:T(8,128)(2,1)S(1)}, u32[]{:S(2)}, u32[]{:S(2)}) collective-permute-start(bf16[80,2048]{1,0:T(8,128)(2,1)S(1)} %get-tuple-element.32), channel_id=1, source_target_pairs={{0,16},{4,20},{8,24},{12,28},{16,0},{20,4},{24,8},{28,12},{1,17},{... | collective-permute-start | bytes 983048 | tf_op jit(solution)/shard_map/ppermute | solution.py:71
  76.7 46.7 %collective-permute-start.16 = (bf16[80,2048]{1,0:T(8,128)(2,1)S(1)}, bf16[80,2048]{1,0:T(8,128)(2,1)S(1)}, u32[]{:S(2)}, u32[]{:S(2)}) collective-permute-start(bf16[80,2048]{1,0:T(8,128)(2,1)S(1)} %get-tuple-element.31), channel_id=1, source_target_pairs={{0,24},{4,28},{8,0},{12,4},{16,8},{20,12},{24,16},{28,20},{1,25},{... | collective-permute-start | bytes 983048 | tf_op jit(solution)/shard_map/ppermute | solution.py:71
  84.6 38.9 %collective-permute-start.18 = (bf16[80,2048]{1,0:T(8,128)(2,1)S(1)}, bf16[80,2048]{1,0:T(8,128)(2,1)S(1)}, u32[]{:S(2)}, u32[]{:S(2)}) collective-permute-start(bf16[80,2048]{1,0:T(8,128)(2,1)S(1)} %get-tuple-element.33), channel_id=1, source_target_pairs={{0,8},{4,12},{8,16},{12,20},{16,24},{20,28},{24,0},{28,4},{1,9},{5... | collective-permute-start | bytes 983048 | tf_op jit(solution)/shard_map/ppermute | solution.py:71
  86.2 51.1 %collective-permute-start.19 = (bf16[80,2048]{1,0:T(8,128)(2,1)S(1)}, bf16[80,2048]{1,0:T(8,128)(2,1)S(1)}, u32[]{:S(2)}, u32[]{:S(2)}) collective-permute-start(bf16[80,2048]{1,0:T(8,128)(2,1)S(1)} %get-tuple-element.35), channel_id=1, source_target_pairs={{0,16},{4,20},{8,24},{12,28},{16,0},{20,4},{24,8},{28,12},{1,17},{... | collective-permute-start | bytes 983048 | tf_op jit(solution)/shard_map/ppermute | solution.py:71
  92.8 44.6 %collective-permute-start.20 = (bf16[80,2048]{1,0:T(8,128)(2,1)S(1)}, bf16[80,2048]{1,0:T(8,128)(2,1)S(1)}, u32[]{:S(2)}, u32[]{:S(2)}) collective-permute-start(bf16[80,2048]{1,0:T(8,128)(2,1)S(1)} %get-tuple-element.34), channel_id=1, source_target_pairs={{0,24},{4,28},{8,0},{12,4},{16,8},{20,12},{24,16},{28,20},{1,25},{... | collective-permute-start | bytes 983048 | tf_op jit(solution)/shard_map/ppermute | solution.py:71
  139.4 13.6 %copy-start.12 = (bf16[320,128]{1,0:T(8,128)(2,1)}, bf16[320,128]{1,0:T(8,128)(2,1)S(1)}, u32[]{:S(2)}) copy-start(bf16[320,128]{1,0:T(8,128)(2,1)S(1)} %get-tuple-element.49) | copy-start | bytes 245764
  139.4 13.6 %copy-start.13 = (bf16[320,128]{1,0:T(8,128)(2,1)}, bf16[320,128]{1,0:T(8,128)(2,1)S(1)}, u32[]{:S(2)}) copy-start(bf16[320,128]{1,0:T(8,128)(2,1)S(1)} %get-tuple-element.50) | copy-start | bytes 245764
  139.4 4.0 %collective-permute-start.5 = (bf16[320,384]{1,0:T(8,128)(2,1)S(1)}, bf16[320,384]{1,0:T(8,128)(2,1)S(1)}, u32[]{:S(2)}, u32[]{:S(2)}) collective-permute-start(bf16[320,384]{1,0:T(8,128)(2,1)S(1)} %pad_maximum_fusion.2), channel_id=1, source_target_pairs={{0,3},{1,0},{2,1},{3,2},{4,7},{5,4},{6,5},{7,6},{8,11},{9,8},{10,9... | collective-permute-start | bytes 737288 | tf_op jit(solution)/shard_map/ppermute | solution.py:187
  141.8 8.8 %collective-permute-start.6 = (bf16[320,384]{1,0:T(8,128)(2,1)S(1)}, bf16[320,384]{1,0:T(8,128)(2,1)S(1)}, u32[]{:S(2)}, u32[]{:S(2)}) collective-permute-start(bf16[320,384]{1,0:T(8,128)(2,1)S(1)} %pad_maximum_fusion.2), channel_id=1, source_target_pairs={{0,2},{1,3},{2,0},{3,1},{4,6},{5,7},{6,4},{7,5},{8,10},{9,11},{10,... | collective-permute-start | bytes 737288 | tf_op jit(solution)/shard_map/ppermute | solution.py:187
  143.2 9.8 %collective-permute-start.7 = (bf16[320,384]{1,0:T(8,128)(2,1)S(1)}, bf16[320,384]{1,0:T(8,128)(2,1)S(1)}, u32[]{:S(2)}, u32[]{:S(2)}) collective-permute-start(bf16[320,384]{1,0:T(8,128)(2,1)S(1)} %pad_maximum_fusion.2), channel_id=1, source_target_pairs={{0,1},{1,2},{2,3},{3,0},{4,5},{5,6},{6,7},{7,4},{8,9},{9,10},{10,1... | collective-permute-start | bytes 737288 | tf_op jit(solution)/shard_map/ppermute | solution.py:187
  167.2 3.3 %copy-start.15 = (bf16[384,320]{1,0:T(8,128)(2,1)S(1)}, bf16[384,320]{1,0:T(8,128)(2,1)}, u32[]{:S(2)}) copy-start(bf16[384,320]{1,0:T(8,128)(2,1)} %get-tuple-element.9) | copy-start | bytes 737284
  168.0 28.2 %collective-permute-start.8 = (bf16[2,320,384]{2,1,0:T(8,128)(2,1)}, bf16[2,320,384]{2,1,0:T(8,128)(2,1)}, u32[]{:S(2)}, u32[]{:S(2)}) collective-permute-start(bf16[2,320,384]{2,1,0:T(8,128)(2,1)} %dynamic-slice_bitcast_fusion), channel_id=1, source_target_pairs={{0,1},{1,0},{2,3},{3,2},{4,5},{5,4},{6,7},{7,6},{8,9},{9,8},{10,11... | collective-permute-start | bytes 1474568 | tf_op jit(solution)/shard_map/ppermute | solution.py:61
  168.3 6.1 %copy-start.3 = (bf16[384,960]{1,0:T(8,128)(2,1)S(1)}, bf16[384,960]{1,0:T(8,128)(2,1)}, u32[]{:S(2)}) copy-start(bf16[384,960]{1,0:T(8,128)(2,1)} %attend_back.1) | copy-start | bytes 2211844
  173.6 4.3 %copy-start.19 = (bf16[4,1,80,384]{3,2,1,0:T(8,128)(2,1)S(1)}, bf16[4,1,80,384]{3,2,1,0:T(8,128)(2,1)}, u32[]{:S(2)}) copy-start(bf16[4,1,80,384]{3,2,1,0:T(8,128)(2,1)} %get-tuple-element.77) | copy-start | bytes 737284
  173.6 5.7 %copy-start.18 = (bf16[4,1,80,384]{3,2,1,0:T(8,128)(2,1)S(1)}, bf16[4,1,80,384]{3,2,1,0:T(8,128)(2,1)}, u32[]{:S(2)}) copy-start(bf16[4,1,80,384]{3,2,1,0:T(8,128)(2,1)} %get-tuple-element.57) | copy-start | bytes 737284
  173.6 14.4 %collective-permute-start.29 = (bf16[4,160,320]{2,1,0:T(8,128)(2,1)}, bf16[4,160,320]{2,1,0:T(8,128)(2,1)}, u32[]{:S(2)}, u32[]{:S(2)}) collective-permute-start(bf16[4,160,320]{2,1,0:T(8,128)(2,1)} %bitcast.250), channel_id=1, source_target_pairs={{0,4},{4,0},{8,12},{12,8},{16,20},{20,16},{24,28},{28,24},{1,5},{5... | collective-permute-start | bytes 1228808 | tf_op jit(solution)/shard_map/ppermute | solution.py:61
  176.7 4.8 %copy-start.17 = (bf16[4,1,80,384]{3,2,1,0:T(8,128)(2,1)S(1)}, bf16[4,1,80,384]{3,2,1,0:T(8,128)(2,1)}, u32[]{:S(2)}) copy-start(bf16[4,1,80,384]{3,2,1,0:T(8,128)(2,1)} %get-tuple-element.56) | copy-start | bytes 737284
  176.7 27.9 %collective-permute-start.21 = (bf16[4,80,960]{2,1,0:T(8,128)(2,1)}, bf16[4,80,960]{2,1,0:T(8,128)(2,1)}, u32[]{:S(2)}, u32[]{:S(2)}) collective-permute-start(bf16[4,80,960]{2,1,0:T(8,128)(2,1)} %bitcast.62), channel_id=1, source_target_pairs={{0,4},{4,0},{8,12},{12,8},{16,20},{20,16},{24,28},{28,24},{1,5},{5... | collective-permute-start | bytes 1843208 | tf_op jit(solution)/shard_map/ppermute | solution.py:61
  179.3 3.5 %copy-start.14 = (bf16[4,1,160,384]{3,2,1,0:T(8,128)(2,1)S(1)}, bf16[4,1,160,384]{3,2,1,0:T(8,128)(2,1)}, u32[]{:S(2)}) copy-start(bf16[4,1,160,384]{3,2,1,0:T(8,128)(2,1)} %get-tuple-element.37) | copy-start | bytes 1474564
  179.3 3.5 %copy-start.16 = (bf16[384,320]{1,0:T(8,128)(2,1)S(1)}, bf16[384,320]{1,0:T(8,128)(2,1)}, u32[]{:S(2)}) copy-start(bf16[384,320]{1,0:T(8,128)(2,1)} %get-tuple-element.9) | copy-start | bytes 737284
  180.7 34.7 %collective-permute-start.25 = (bf16[4,80,960]{2,1,0:T(8,128)(2,1)}, bf16[4,80,960]{2,1,0:T(8,128)(2,1)}, u32[]{:S(2)}, u32[]{:S(2)}) collective-permute-start(bf16[4,80,960]{2,1,0:T(8,128)(2,1)} %bitcast.71), channel_id=1, source_target_pairs={{0,4},{4,0},{8,12},{12,8},{16,20},{20,16},{24,28},{28,24},{1,5},{5... | collective-permute-start | bytes 1843208 | tf_op jit(solution)/shard_map/ppermute | solution.py:61
  188.0 9.5 %copy-start.7 = (bf16[1280,384]{1,0:T(8,128)(2,1)S(1)}, bf16[1280,384]{1,0:T(8,128)(2,1)}, u32[]{:S(2)}) copy-start(bf16[1280,384]{1,0:T(8,128)(2,1)} %copy-done.6) | copy-start | bytes 2949124
  189.3 15.2 %copy-start.11 = (bf16[320,960]{1,0:T(8,128)(2,1)S(1)}, bf16[320,960]{1,0:T(8,128)(2,1)}, u32[]{:S(2)}) copy-start(bf16[320,960]{1,0:T(8,128)(2,1)} %convolution_convert_fusion.10) | copy-start | bytes 1843204
  189.4 10.5 %collective-permute-start.30 = (bf16[160,320]{1,0:T(8,128)(2,1)S(1)}, bf16[160,320]{1,0:T(8,128)(2,1)S(1)}, u32[]{:S(2)}, u32[]{:S(2)}) collective-permute-start(bf16[160,320]{1,0:T(8,128)(2,1)S(1)} %get-tuple-element.51), channel_id=1, source_target_pairs={{0,8},{4,12},{8,16},{12,20},{16,24},{20,28},{24,0},{28,4},{1,9},{5... | collective-permute-start | bytes 307208 | tf_op jit(solution)/shard_map/ppermute | solution.py:71
  195.1 8.6 %collective-permute-start.31 = (bf16[160,320]{1,0:T(8,128)(2,1)S(1)}, bf16[160,320]{1,0:T(8,128)(2,1)S(1)}, u32[]{:S(2)}, u32[]{:S(2)}) collective-permute-start(bf16[160,320]{1,0:T(8,128)(2,1)S(1)} %get-tuple-element.53), channel_id=1, source_target_pairs={{0,16},{4,20},{8,24},{12,28},{16,0},{20,4},{24,8},{28,12},{1,17},{... | collective-permute-start | bytes 307208 | tf_op jit(solution)/shard_map/ppermute | solution.py:71
  196.2 7.6 %collective-permute-start.32 = (bf16[160,320]{1,0:T(8,128)(2,1)S(1)}, bf16[160,320]{1,0:T(8,128)(2,1)S(1)}, u32[]{:S(2)}, u32[]{:S(2)}) collective-permute-start(bf16[160,320]{1,0:T(8,128)(2,1)S(1)} %get-tuple-element.52), channel_id=1, source_target_pairs={{0,24},{4,28},{8,0},{12,4},{16,8},{20,12},{24,16},{28,20},{1,25},{... | collective-permute-start | bytes 307208 | tf_op jit(solution)/shard_map/ppermute | solution.py:71
  199.9 18.0 %collective-permute-start.9 = (bf16[320,384]{1,0:T(8,128)(2,1)S(1)}, bf16[320,384]{1,0:T(8,128)(2,1)S(1)}, u32[]{:S(2)}, u32[]{:S(2)}) collective-permute-start(bf16[320,384]{1,0:T(8,128)(2,1)S(1)} %fusion.14), channel_id=1, source_target_pairs={{0,2},{1,3},{2,0},{3,1},{4,6},{5,7},{6,4},{7,5},{8,10},{9,11},{10,... | collective-permute-start | bytes 737288 | tf_op jit(solution)/shard_map/ppermute | solution.py:71
  204.6 10.9 %copy-start.10 = (bf16[320,960]{1,0:T(8,128)(2,1)S(1)}, bf16[320,960]{1,0:T(8,128)(2,1)}, u32[]{:S(2)}) copy-start(bf16[320,960]{1,0:T(8,128)(2,1)} %convolution_convert_fusion.8) | copy-start | bytes 1843204
  207.9 10.0 %copy-start.9 = (bf16[384,320]{0,1:T(8,128)(2,1)S(1)}, bf16[384,320]{0,1:T(8,128)(2,1)}, u32[]{:S(2)}) copy-start(bf16[384,320]{0,1:T(8,128)(2,1)} %param.13) | copy-start | bytes 737284
  207.9 40.4 %collective-permute-start.22 = (bf16[80,960]{1,0:T(8,128)(2,1)}, bf16[80,960]{1,0:T(8,128)(2,1)}, u32[]{:S(2)}, u32[]{:S(2)}) collective-permute-start(bf16[80,960]{1,0:T(8,128)(2,1)} %get-tuple-element.42), channel_id=1, source_target_pairs={{0,8},{4,12},{8,16},{12,20},{16,24},{20,28},{24,0},{28,4},{1,9},{5... | collective-permute-start | bytes 460808 | tf_op jit(solution)/shard_map/ppermute | solution.py:71
  211.1 39.3 %collective-permute-start.23 = (bf16[80,960]{1,0:T(8,128)(2,1)}, bf16[80,960]{1,0:T(8,128)(2,1)}, u32[]{:S(2)}, u32[]{:S(2)}) collective-permute-start(bf16[80,960]{1,0:T(8,128)(2,1)} %get-tuple-element.44), channel_id=1, source_target_pairs={{0,16},{4,20},{8,24},{12,28},{16,0},{20,4},{24,8},{28,12},{1,17},{... | collective-permute-start | bytes 460808 | tf_op jit(solution)/shard_map/ppermute | solution.py:71
  217.9 2.6 copy-start.22
  218.2 2.3 collective-permute-start.10
  218.4 3.7 %collective-permute-start.11 = (f32[1088]{0:T(1024)S(1)}, f32[1088]{0:T(1024)S(1)}, u32[]{:S(2)}, u32[]{:S(2)}) collective-permute-start(f32[1088]{0:T(1024)S(1)} %pad_maximum_fusion.3), channel_id=1, source_target_pairs={{0,2},{1,3},{2,0},{3,1},{4,6},{5,7},{6,4},{7,5},{8,10},{9,11},{10,... | collective-permute-start | bytes 13064 | tf_op jit(solution)/shard_map/ppermute | solution.py:187
  219.5 3.1 %collective-permute-start.12 = (f32[1088]{0:T(1024)S(1)}, f32[1088]{0:T(1024)S(1)}, u32[]{:S(2)}, u32[]{:S(2)}) collective-permute-start(f32[1088]{0:T(1024)S(1)} %pad_maximum_fusion.3), channel_id=1, source_target_pairs={{0,1},{1,2},{2,3},{3,0},{4,5},{5,6},{6,7},{7,4},{8,9},{9,10},{10,1... | collective-permute-start | bytes 13064 | tf_op jit(solution)/shard_map/ppermute | solution.py:187
  226.2 10.8 %collective-permute-start.33 = (bf16[160]{0:T(256)(128)(2,1)S(1)}, bf16[160]{0:T(256)(128)(2,1)S(1)}, u32[]{:S(2)}, u32[]{:S(2)}) collective-permute-start(bf16[160]{0:T(256)(128)(2,1)S(1)} %get-tuple-element.13), channel_id=1, source_target_pairs={{0,4},{4,8},{8,12},{12,16},{16,20},{20,24},{24,28},{28,0},{1,5},{5... | collective-permute-start | bytes 968 | tf_op jit(solution)/shard_map/ppermute | solution.py:93
  227.0 12.3 %collective-permute-start.34 = (bf16[160]{0:T(256)(128)(2,1)S(1)}, bf16[160]{0:T(256)(128)(2,1)S(1)}, u32[]{:S(2)}, u32[]{:S(2)}) collective-permute-start(bf16[160]{0:T(256)(128)(2,1)S(1)} %get-tuple-element.19), channel_id=1, source_target_pairs={{0,8},{4,12},{8,16},{12,20},{16,24},{20,28},{24,0},{28,4},{1,9},{5... | collective-permute-start | bytes 968 | tf_op jit(solution)/shard_map/ppermute | solution.py:93
  233.4 7.7 %collective-permute-start.35 = (bf16[160]{0:T(256)(128)(2,1)S(1)}, bf16[160]{0:T(256)(128)(2,1)S(1)}, u32[]{:S(2)}, u32[]{:S(2)}) collective-permute-start(bf16[160]{0:T(256)(128)(2,1)S(1)} %get-tuple-element.18), channel_id=1, source_target_pairs={{0,12},{4,16},{8,20},{12,24},{16,28},{20,0},{24,4},{28,8},{1,13},{... | collective-permute-start | bytes 968 | tf_op jit(solution)/shard_map/ppermute | solution.py:93
  237.0 4.7 %collective-permute-start.36 = (bf16[160]{0:T(256)(128)(2,1)S(1)}, bf16[160]{0:T(256)(128)(2,1)S(1)}, u32[]{:S(2)}, u32[]{:S(2)}) collective-permute-start(bf16[160]{0:T(256)(128)(2,1)S(1)} %get-tuple-element.17), channel_id=1, source_target_pairs={{0,16},{4,20},{8,24},{12,28},{16,0},{20,4},{24,8},{28,12},{1,17},{... | collective-permute-start | bytes 968 | tf_op jit(solution)/shard_map/ppermute | solution.py:93
  239.3 4.5 %collective-permute-start.37 = (bf16[160]{0:T(256)(128)(2,1)S(1)}, bf16[160]{0:T(256)(128)(2,1)S(1)}, u32[]{:S(2)}, u32[]{:S(2)}) collective-permute-start(bf16[160]{0:T(256)(128)(2,1)S(1)} %get-tuple-element.16), channel_id=1, source_target_pairs={{0,20},{4,24},{8,28},{12,0},{16,4},{20,8},{24,12},{28,16},{1,21},{... | collective-permute-start | bytes 968 | tf_op jit(solution)/shard_map/ppermute | solution.py:93
  241.1 4.9 %collective-permute-start.38 = (bf16[160]{0:T(256)(128)(2,1)S(1)}, bf16[160]{0:T(256)(128)(2,1)S(1)}, u32[]{:S(2)}, u32[]{:S(2)}) collective-permute-start(bf16[160]{0:T(256)(128)(2,1)S(1)} %get-tuple-element.15), channel_id=1, source_target_pairs={{0,24},{4,28},{8,0},{12,4},{16,8},{20,12},{24,16},{28,20},{1,25},{... | collective-permute-start | bytes 968 | tf_op jit(solution)/shard_map/ppermute | solution.py:93
  241.7 4.2 %collective-permute-start.39 = (bf16[160]{0:T(256)(128)(2,1)S(1)}, bf16[160]{0:T(256)(128)(2,1)S(1)}, u32[]{:S(2)}, u32[]{:S(2)}) collective-permute-start(bf16[160]{0:T(256)(128)(2,1)S(1)} %get-tuple-element.14), channel_id=1, source_target_pairs={{0,28},{4,0},{8,4},{12,8},{16,12},{20,16},{24,20},{28,24},{1,29},{... | collective-permute-start | bytes 968 | tf_op jit(solution)/shard_map/ppermute | solution.py:93
  243.8 11.2 %collective-permute-start.24 = (bf16[80,960]{1,0:T(8,128)(2,1)}, bf16[80,960]{1,0:T(8,128)(2,1)S(1)}, u32[]{:S(2)}, u32[]{:S(2)}) collective-permute-start(bf16[80,960]{1,0:T(8,128)(2,1)} %get-tuple-element.43), channel_id=1, source_target_pairs={{0,24},{4,28},{8,0},{12,4},{16,8},{20,12},{24,16},{28,20},{1,25},{... | collective-permute-start | bytes 460808 | tf_op jit(solution)/shard_map/ppermute | solution.py:71
  246.0 10.3 %collective-permute-start.26 = (bf16[80,960]{1,0:T(8,128)(2,1)}, bf16[80,960]{1,0:T(8,128)(2,1)S(1)}, u32[]{:S(2)}, u32[]{:S(2)}) collective-permute-start(bf16[80,960]{1,0:T(8,128)(2,1)} %get-tuple-element.45), channel_id=1, source_target_pairs={{0,8},{4,12},{8,16},{12,20},{16,24},{20,28},{24,0},{28,4},{1,9},{5... | collective-permute-start | bytes 460808 | tf_op jit(solution)/shard_map/ppermute | solution.py:71
  246.0 14.4 %collective-permute-start.27 = (bf16[80,960]{1,0:T(8,128)(2,1)}, bf16[80,960]{1,0:T(8,128)(2,1)S(1)}, u32[]{:S(2)}, u32[]{:S(2)}) collective-permute-start(bf16[80,960]{1,0:T(8,128)(2,1)} %get-tuple-element.47), channel_id=1, source_target_pairs={{0,16},{4,20},{8,24},{12,28},{16,0},{20,4},{24,8},{28,12},{1,17},{... | collective-permute-start | bytes 460808 | tf_op jit(solution)/shard_map/ppermute | solution.py:71
  248.2 12.1 %collective-permute-start.28 = (bf16[80,960]{1,0:T(8,128)(2,1)}, bf16[80,960]{1,0:T(8,128)(2,1)S(1)}, u32[]{:S(2)}, u32[]{:S(2)}) collective-permute-start(bf16[80,960]{1,0:T(8,128)(2,1)} %get-tuple-element.46), channel_id=1, source_target_pairs={{0,24},{4,28},{8,0},{12,4},{16,8},{20,12},{24,16},{28,20},{1,25},{... | collective-permute-start | bytes 460808 | tf_op jit(solution)/shard_map/ppermute | solution.py:71
  (4 other events, 5.3 us)
where the time goes:
time: 264 us; the launch traced here: 263 us
  waiting for transfers between devices  82.3 us (31%)
  starting transfers between devices  65 us (25%)
  local copies, waits for them, and re-layouts  36.4 us (14%)
  other arithmetic  32 us (12%)
  matrix products  29.5 us (11%)
  Pallas kernels  14.7 us (6%)
  between operations  3 us (1%)
    ppermute x24, waiting for transfers between devices, two_stage_sum(): arrived.append(lax.ppermute(sent, axis, pairs))  70.2 us
    ppermute x24, starting transfers between devices, two_stage_sum(): arrived.append(lax.ppermute(sent, axis, pairs))  37.8 us
    dot_general x10, matrix products, term(): jnp.dot(flat, right, preferred_element_type=jnp.float32)  18.2 us
    ppermute x7, starting transfers between devices, small_sum(): summed += lax.ppermute(sent, axis, pairs).astype(jnp.float32)  15 us
    unnamed x67, local copies, waits for them, and re-layouts  12.9 us
    ppermute x9, waiting for transfers between devices, gathered(): stacked.append(lax.ppermute(share, axis, pairs))  11.5 us
    add x6, other arithmetic, two_stage_sum(): running += value.astype(jnp.float32)  11.4 us
    dot_general x2, matrix products, two_stage_sum(): jnp.dot(left.reshape(-1, left.shape[2]), right, preferred_element_type=jn...  9.16 us
  transfers between devices with their start and end apart: 41, of which 16 were waited for; matrix products, arithmetic and copies ran while one was open for 32% of the time, Pallas kernels for 3%

commit v1 on v0

--- a/solution.py
+++ b/solution.py
@@ -35,21 +35,17 @@
     return lax.dynamic_index_in_dim(values, place, dim, keepdims=False, allow_negative_indices=False)
 
 
-def two_stage_sum(left, right, axis, inner, whole=False):
+def two_stage_sum(left, right, axis, inner):
     total = left.shape[0]
     outer = total // inner
     index = lax.axis_index(axis).astype(jnp.uint32)
     at_outer, at_inner = lax.div(index, jnp.uint32(inner)), lax.rem(index, jnp.uint32(inner))
     lefts = left.reshape((outer, inner) + left.shape[1:])
 
-    if whole:
-        every = jnp.dot(left.reshape(-1, left.shape[2]), right, preferred_element_type=jnp.float32)
-        every = every.astype(jnp.bfloat16).reshape((outer, inner) + (left.shape[1], right.shape[1]))
-
     def term(place):
-        if whole:
-            return pick(every, place, 1)
         chosen = pick(lefts, place, 1)
+        if right is None:
+            return chosen
         flat = chosen.reshape(-1, chosen.shape[-1])
         product = jnp.dot(flat, right, preferred_element_type=jnp.float32).astype(jnp.bfloat16)
         return product.reshape(outer, -1, right.shape[1])
@@ -83,17 +79,6 @@
     return jnp.concatenate(pieces, axis=0) if cuts > 1 else pieces[0]
 
 
-def small_sum(part, axis):
-    total = part.shape[0]
-    index = lax.axis_index(axis).astype(jnp.uint32)
-    summed = pick(part, index, 0).astype(jnp.float32)
-    for step in range(1, total):
-        pairs = [(i, (i + step) % total) for i in range(total)]
-        sent = pick(part, lax.rem(index + jnp.uint32(step), jnp.uint32(total)), 0)
-        summed += lax.ppermute(sent, axis, pairs).astype(jnp.float32)
-    return summed
-
-
 def attend_kernel(size, counts_ref, packed_ref, prob_ref, mixed_ref):
     tile = packed_ref.shape[0]
     count = counts_ref[pl.program_id(0)]
@@ -137,7 +122,7 @@
     )(counts, packed)
 
 
-def attend_back_kernel(size, packed_ref, prob_ref, vis_ref, out_ref, grad_ref):
+def attend_back_kernel(size, packed_ref, prob_ref, vis_ref, out_ref, qkv_ref, grad_ref, part_ref):
     scaling = 1.0 / size**0.5
     mixed_grads = lax.dot_general(
         vis_ref[...], out_ref[...], (((0,), (1,)), ((), ())), preferred_element_type=jnp.float32
@@ -157,9 +142,10 @@
         grad_ref[:, base : base + size] = q_grad.astype(jnp.bfloat16)
         grad_ref[:, base + size : base + 2 * size] = dot_tn(score_grad, queries).astype(jnp.bfloat16)
         grad_ref[:, base + 2 * size : base + 3 * size] = dot_tn(prob_low, mixed_grad).astype(jnp.bfloat16)
-
-
-def attend_back(packed, probability, vis_low, w_out, size):
+    part_ref[...] = dot_nt(qkv_ref[...], grad_ref[...]).astype(jnp.bfloat16)
+
+
+def attend_back(packed, probability, vis_low, w_out, qkv_flat, size):
     rows, width = packed.shape
     images, heads = probability.shape[:2]
     return pl.pallas_call(
@@ -170,12 +156,19 @@
             pl.BlockSpec((1, heads, TILE, TILE), lambda i: (i, 0, 0, 0)),
             pl.BlockSpec((vis_low.shape[0], TILE), lambda i: (0, i)),
             pl.BlockSpec(w_out.shape, lambda i: (0, 0)),
-        ],
-        out_specs=pl.BlockSpec((TILE, width), lambda i: (i, 0)),
-        out_shape=jax.ShapeDtypeStruct((rows, width), jnp.bfloat16),
+            pl.BlockSpec(qkv_flat.shape, lambda i: (0, 0)),
+        ],
+        out_specs=[
+            pl.BlockSpec((TILE, width), lambda i: (i, 0)),
+            pl.BlockSpec((vis_low.shape[0], TILE), lambda i: (0, i)),
+        ],
+        out_shape=[
+            jax.ShapeDtypeStruct((rows, width), jnp.bfloat16),
+            jax.ShapeDtypeStruct(vis_low.shape, jnp.bfloat16),
+        ],
         cost_estimate=pl.CostEstimate(flops=3 * 10**9, bytes_accessed=6 * 10**6, transcendentals=0),
         name="attend_back",
-    )(packed, probability, vis_low, w_out)
+    )(packed, probability, vis_low, w_out, qkv_flat)
 
 
 def gathered(share, axis):
@@ -221,7 +214,8 @@
     piece_rows = features_dim // groups
     grad_proj = summed_rows(kept_rows.T.reshape(groups, piece_rows, block_rows), grad_rows, "enc", inner, 2)
 
-    shared = two_stage_sum(w_proj.reshape(tp_size, share_width, w_proj.shape[1]), grad_rows.T, "tp", 2, whole=True)
+    vis_part = dot_nt(w_proj, grad_rows).astype(jnp.bfloat16)
+    shared = two_stage_sum(vis_part.reshape(tp_size, share_width, block_rows), None, "tp", 2)
     tiles = jnp.where(live_own.reshape(-1)[None, :], shared, 0.0).astype(jnp.bfloat16)
     tiles = [tiles[:, j * TILE : (j + 1) * TILE] for j in range(img_group)]
     outgoing = jnp.zeros((groups, share_width, TILE), jnp.bfloat16)
@@ -243,11 +237,9 @@
     normed_in = (centred * inverse1 * ln1_gain[:, None]).astype(jnp.bfloat16)
     packed = dot_tn(normed_in, qkv_flat).astype(jnp.bfloat16)
     probability, mixed = attend(packed, arrived_counts, heads_here, head_size)
-    packed_grad = attend_back(packed, probability, vis_low, w_out, head_size)
-
-    in_sum = two_stage_sum(
-        qkv_flat.reshape(tp_size, share_width, qkv_flat.shape[1]), packed_grad.T, "tp", 2, whole=True
-    )
+    packed_grad, in_part = attend_back(packed, probability, vis_low, w_out, qkv_flat, head_size)
+
+    in_sum = two_stage_sum(in_part.reshape(tp_size, share_width, block_rows), None, "tp", 2)
     normed_share = (block_turned.astype(jnp.float32) - centre) * inverse1
     gain_share = lax.dynamic_slice_in_dim(ln1_gain, tp_rank * share_width, share_width, 0)
     scaled = in_sum * gain_share[:, None]
@@ -262,9 +254,12 @@
     grad_qkv = summed_rows(
         normed_in.reshape(groups, piece_rows, block_rows), packed_grad, "enc", inner, 2
     ).reshape(piece_rows, heads_here, 3 * head_size)
-    grad_out = two_stage_sum(vis_low.reshape(groups, piece_rows, block_rows), mixed, "enc", inner).T
-    ln1_term = small[:, 2 * block_rows :].reshape(groups, piece_rows).astype(jnp.bfloat16)
-    grad_ln1 = small_sum(ln1_term, "enc")
+    out_term = jnp.dot(vis_low, mixed, preferred_element_type=jnp.float32).astype(jnp.bfloat16)
+    ln1_term = small[:, 2 * block_rows :].reshape(features_dim, 1).astype(jnp.bfloat16)
+    both = jnp.concatenate([out_term, ln1_term], axis=1)
+    both = two_stage_sum(both.reshape(groups, piece_rows, -1), None, "enc", inner)
+    grad_out = both[:, :-1].T
+    grad_ln1 = both[:, -1]
     return (grad_input, grad_proj, grad_qkv, grad_out, grad_ln1)
 
 

time: 264 us -> 247 us (0.936)
  waiting for transfers between devices: 82.3 us -> 97 us
  starting transfers between devices: 65 us -> 54.1 us
  matrix products: 29.5 us -> 20.2 us
  local copies, waits for them, and re-layouts: 36.4 us -> 27.3 us
  other arithmetic: 32 us -> 25.9 us
  Pallas kernels: 14.7 us -> 18.2 us
    ppermute x24, waiting for transfers between devices: 70.2 us -> 86.5 us  [two_stage_sum(): arrived.append(lax.ppermute(sent, axis, pairs))]
    ppermute x7 -> x0, starting transfers between devices: 15 us -> none  [small_sum(): summed += lax.ppermute(sent, axis, pairs).astype(jnp.float32)]
    dot_general x10 -> x8, matrix products: 18.2 us -> 11.9 us  [term(): jnp.dot(flat, right, preferred_element_type=jnp.float32)]
    unnamed x67 -> x77, local copies, waits for them, and re-layouts: 12.9 us -> 7.97 us
    reshape x0 -> x1, local copies, waits for them, and re-layouts: none -> 4.52 us  [shards(): qkv_flat = w_qkv.reshape(features_dim, heads_here * 3 * head_size)]
    ppermute x24, starting transfers between devices: 37.8 us -> 41.9 us  [two_stage_sum(): arrived.append(lax.ppermute(sent, axis, pairs))]
    convert_element_type x4 -> x2, local copies, waits for them, and re-layouts: 5.13 us -> 1.22 us  [the longest x1 0.64 us: shards(): jnp.dot(vis_low, mixed, preferred_element_type=jnp.float32)]
    add x6, other arithmetic: 11.4 us -> 7.71 us  [two_stage_sum(): running += value.astype(jnp.float32)]
  transfers between devices with their start and end apart: 41 -> 34, of which waited for: 16 -> 13; matrix products, arithmetic and copies ran while one was open for 32% -> 26% of each run, Pallas kernels for 3% -> 3%
where the time goes in v1:
time: 247 us; the launch traced here: 246 us
  waiting for transfers between devices  97 us (39%)
  starting transfers between devices  54.1 us (22%)
  local copies, waits for them, and re-layouts  27.3 us (11%)
  other arithmetic  25.9 us (10%)
  matrix products  20.2 us (8%)
  Pallas kernels  18.2 us (7%)
  between operations  3.28 us (1%)
    ppermute x24, waiting for transfers between devices, two_stage_sum(): arrived.append(lax.ppermute(sent, axis, pairs))  86.5 us
    ppermute x24, starting transfers between devices, two_stage_sum(): arrived.append(lax.ppermute(sent, axis, pairs))  41.9 us
    dot_general x8, matrix products, term(): jnp.dot(flat, right, preferred_element_type=jnp.float32)  11.9 us
    pallas_call x1, Pallas kernels, attend_back(): pl.pallas_call(lambda *refs: attend_back_kernel(size, *refs), grid=(image...  11.6 us
    ppermute x9, waiting for transfers between devices, gathered(): stacked.append(lax.ppermute(share, axis, pairs))  10.5 us
    unnamed x77, local copies, waits for them, and re-layouts  7.97 us
    add x6, other arithmetic, two_stage_sum(): running += value.astype(jnp.float32)  7.71 us
    pallas_call x1, Pallas kernels, attend(): pl.pallas_call(lambda *refs: attend_kernel(size, *refs), grid=(images,),...  6.65 us
  transfers between devices with their start and end apart: 34, of which 13 were waited for; matrix products, arithmetic and copies ran while one was open for 26% of the time, Pallas kernels for 3%

profile of v1, /device:TPU:0, one launch (start us, length us, event | category | flops | bytes accessed | tf_op | source)
XLA Modules:
  0.0 246.0 jit_solution(428868368759773516)
XLA Ops:
  0.6 2.5 %collective-permute-start.2 = (bf16[320,384]{1,0:T(8,128)(2,1)}, bf16[320,384]{1,0:T(8,128)(2,1)}, u32[]{:S(2)}, u32[]{:S(2)}) collective-permute-start(bf16[320,384]{1,0:T(8,128)(2,1)} %bitcast.219), channel_id=1, source_target_pairs={{0,3},{1,0},{2,1},{3,2},{4,7},{5,4},{6,5},{7,6},{8,11},{9,8},{10,9... | collective-permute-start | bytes 737288 | tf_op jit(solution)/shard_map/ppermute | solution.py:180
  3.9 5.5 %convolution_convert_fusion = bf16[1280,384]{1,0:T(8,128)(2,1)S(1)} fusion(bf16[1280,2048]{1,0:T(8,128)(2,1)} %param.19, bf16[384,2048]{1,0:T(8,128)(2,1)S(1)} %copy-done), kind=kOutput, calls=%fused_computation.2 | convolution fusion | flops 2013757440 | bytes 7798784 | tf_op jit(solution)/shard_map/dot_general | solution.py:16
  11.2 1.4 collective-permute-start
  14.6 2.0 convolution_convert_fusion.4
  16.6 1.5 collective-permute-start.13
  18.7 1.4 reduce-window.8
  23.7 3.0 %convolution_convert_fusion.5 = bf16[320,2048]{1,0:T(8,128)(2,1)} fusion(bf16[320,384]{1,0:T(8,128)(2,1)} %bitcast.232, bf16[384,2048]{1,0:T(8,128)(2,1)S(1)} %copy-done), kind=kOutput, calls=%fused_computation.7 | convolution fusion | flops 503971840 | bytes 3129344 | tf_op jit(solution)/shard_map/dot_general | solution.py:50
  26.7 1.9 convolution_convert_fusion.2
  28.6 1.9 convolution_convert_fusion.3
  30.6 1.7 iota_compare_fusion.2
  33.8 1.4 fusion.19.refs_0_
  37.8 4.5 %copy.46.refs_4_ = bf16[1280,960]{1,0:T(8,128)(2,1)} copy(bf16[1280,960]{0,1:T(8,128)(2,1)} %bitcast.224) | data formatting | bytes 4915200 | tf_op jit(solution)/shard_map/reshape | solution.py:232
  42.9 1.0 bitcast_dynamic-update-slice_fusion.12
  43.9 1.0 bitcast_dynamic-update-slice_fusion.10
  44.9 1.0 bitcast_dynamic-update-slice_fusion.9
  46.0 1.0 bitcast_dynamic-update-slice_fusion.13
  47.0 1.0 bitcast_dynamic-update-slice_fusion.11
  49.4 1.2 copy-done.7
  50.7 2.1 convolution_convert_fusion.6.refs_1_.refs_0_
  52.8 1.1 convert_add_fusion.6
  55.6 6.6 %attend.1 = (f32[3,4,128,128]{3,2,1,0:T(8,128)}, bf16[384,320]{1,0:T(8,128)(2,1)}) custom-call(s32[3]{0:T(128)} %fusion.19.refs_0_, bf16[384,960]{1,0:T(8,128)(2,1)} %convolution_convert_fusion.6.refs_1_.refs_0_), custom_call_target="tpu_custom_call" | custom-call | flops 2000000000 | bytes 4000000 | tf_op jit(solution)/shard_map/attend/pallas_call | solution.py:105
  62.4 1.1 select_select_fusion
  63.5 5.8 %all-to-all-start = ((bf16[8,320,128]{2,1,0:T(8,128)(2,1)}), bf16[8,320,128]{2,1,0:T(8,128)(2,1)S(1)}, u32[]{:S(2)}, u32[]{:S(2)}) async-start(bf16[8,320,128]{2,1,0:T(8,128)(2,1)} %select_select_fusion), calls=%async_computation | async-start | bytes 1310720 | tf_op jit(solution)/shard_map/all_to_all | solution.py:224
  69.3 1.9 convert_add_fusion.1
  71.3 2.1 collective-permute-start.14
  73.4 2.4 collective-permute-start.15
  75.7 1.5 collective-permute-start.16
  77.2 3.7 %collective-permute-done.17 = bf16[4,80,2048]{2,1,0:T(8,128)(2,1)} collective-permute-done((bf16[4,80,2048]{2,1,0:T(8,128)(2,1)}, bf16[4,80,2048]{2,1,0:T(8,128)(2,1)}, u32[]{:S(2)}, u32[]{:S(2)}) %collective-permute-start.17) | collective-permute-done | bytes 1310752 | tf_op jit(solution)/shard_map/ppermute | solution.py:57
  80.9 1.9 convert_add_fusion
  83.5 4.5 %collective-permute-start.19 = (bf16[80,2048]{1,0:T(8,128)(2,1)S(1)}, bf16[80,2048]{1,0:T(8,128)(2,1)S(1)}, u32[]{:S(2)}, u32[]{:S(2)}) collective-permute-start(bf16[80,2048]{1,0:T(8,128)(2,1)S(1)} %get-tuple-element.32), channel_id=1, source_target_pairs={{0,16},{4,20},{8,24},{12,28},{16,0},{20,4},{24,8},{28,12},{1,17},{... | collective-permute-start | bytes 983048 | tf_op jit(solution)/shard_map/ppermute | solution.py:67
  88.0 4.5 %collective-permute-done.14 = bf16[80,2048]{1,0:T(8,128)(2,1)S(1)} collective-permute-done((bf16[80,2048]{1,0:T(8,128)(2,1)S(1)}, bf16[80,2048]{1,0:T(8,128)(2,1)S(1)}, u32[]{:S(2)}, u32[]{:S(2)}) %collective-permute-start.14) | collective-permute-done | bytes 327712 | tf_op jit(solution)/shard_map/ppermute | solution.py:67
  92.4 30.5 %collective-permute-done.15 = bf16[80,2048]{1,0:T(8,128)(2,1)S(1)} collective-permute-done((bf16[80,2048]{1,0:T(8,128)(2,1)S(1)}, bf16[80,2048]{1,0:T(8,128)(2,1)S(1)}, u32[]{:S(2)}, u32[]{:S(2)}) %collective-permute-start.15) | collective-permute-done | bytes 327712 | tf_op jit(solution)/shard_map/ppermute | solution.py:67
  123.2 13.9 %collective-permute-done.19 = bf16[80,2048]{1,0:T(8,128)(2,1)S(1)} collective-permute-done((bf16[80,2048]{1,0:T(8,128)(2,1)S(1)}, bf16[80,2048]{1,0:T(8,128)(2,1)S(1)}, u32[]{:S(2)}, u32[]{:S(2)}) %collective-permute-start.19) | collective-permute-done | bytes 327712 | tf_op jit(solution)/shard_map/ppermute | solution.py:67
  137.4 1.1 pad_maximum_fusion
  138.5 1.4 collective-permute-start.6
  140.2 1.4 collective-permute-done.5
  141.7 7.8 %collective-permute-done.6 = bf16[320,384]{1,0:T(8,128)(2,1)S(1)} collective-permute-done((bf16[320,384]{1,0:T(8,128)(2,1)S(1)}, bf16[320,384]{1,0:T(8,128)(2,1)S(1)}, u32[]{:S(2)}, u32[]{:S(2)}) %collective-permute-start.6) | collective-permute-done | bytes 245792 | tf_op jit(solution)/shard_map/ppermute | solution.py:180
  149.5 1.3 collective-permute-done.7
  153.2 11.6 %attend_back.1 = (bf16[384,960]{1,0:T(8,128)(2,1)}, bf16[1280,384]{1,0:T(8,128)(2,1)}) custom-call(bf16[384,960]{1,0:T(8,128)(2,1)} %convolution_convert_fusion.6.refs_1_.refs_0_, f32[3,4,128,128]{3,2,1,0:T(8,128)} %get-tuple-element.10.refs_1_, bf16[1280,384]{1,0:T(8,128)(2,1)} %bitcast.217, bf16[320,1280]{1,0:T(8,128)(2,1)} %refs_3_.1, ...), custom_call_target="tpu_custom_call" | custom-call | flops 3000000000 | bytes 6000000 | tf_op jit(solution)/shard_map/attend_back/pallas_call | solution.py:151
  164.7 1.2 dynamic-slice_bitcast_fusion
  166.0 1.6 convolution_convert_fusion.9
  169.0 1.3 collective-permute-start.25
  172.2 13.1 %collective-permute-done.21 = bf16[4,80,960]{2,1,0:T(8,128)(2,1)S(1)} collective-permute-done((bf16[4,80,960]{2,1,0:T(8,128)(2,1)S(1)}, bf16[4,80,960]{2,1,0:T(8,128)(2,1)S(1)}, u32[]{:S(2)}, u32[]{:S(2)}) %collective-permute-start.21) | collective-permute-done | bytes 614432 | tf_op jit(solution)/shard_map/ppermute | solution.py:57
  185.3 1.4 convert_add_fusion.3
  187.5 5.7 %collective-permute-start.22 = (bf16[80,960]{1,0:T(8,128)(2,1)}, bf16[80,960]{1,0:T(8,128)(2,1)}, u32[]{:S(2)}, u32[]{:S(2)}) collective-permute-start(bf16[80,960]{1,0:T(8,128)(2,1)} %get-tuple-element.37), channel_id=1, source_target_pairs={{0,8},{4,12},{8,16},{12,20},{16,24},{20,28},{24,0},{28,4},{1,9},{5... | collective-permute-start | bytes 460808 | tf_op jit(solution)/shard_map/ppermute | solution.py:67
  193.2 1.1 collective-permute-start.23
  194.3 4.6 %collective-permute-done.25 = bf16[4,80,960]{2,1,0:T(8,128)(2,1)S(1)} collective-permute-done((bf16[4,80,960]{2,1,0:T(8,128)(2,1)S(1)}, bf16[4,80,960]{2,1,0:T(8,128)(2,1)S(1)}, u32[]{:S(2)}, u32[]{:S(2)}) %collective-permute-start.25) | collective-permute-done | bytes 614432 | tf_op jit(solution)/shard_map/ppermute | solution.py:57
  198.9 1.3 convert_add_fusion.2
  200.6 1.4 collective-permute-start.11
  202.7 6.7 %collective-permute-start.24 = (bf16[80,960]{1,0:T(8,128)(2,1)}, bf16[80,960]{1,0:T(8,128)(2,1)S(1)}, u32[]{:S(2)}, u32[]{:S(2)}) collective-permute-start(bf16[80,960]{1,0:T(8,128)(2,1)} %get-tuple-element.38), channel_id=1, source_target_pairs={{0,24},{4,28},{8,0},{12,4},{16,8},{20,12},{24,16},{28,20},{1,25},{... | collective-permute-start | bytes 460808 | tf_op jit(solution)/shard_map/ppermute | solution.py:67
  210.1 2.3 collective-permute-start.27
  212.5 1.9 fusion.14
  215.2 1.0 collective-permute-start.28
  216.2 1.7 collective-permute-start.29
  218.0 1.2 fusion.13
  219.2 6.4 %collective-permute-done.27 = bf16[80,960]{1,0:T(8,128)(2,1)S(1)} collective-permute-done((bf16[80,960]{1,0:T(8,128)(2,1)S(1)}, bf16[80,960]{1,0:T(8,128)(2,1)S(1)}, u32[]{:S(2)}, u32[]{:S(2)}) %collective-permute-start.27) | collective-permute-done | bytes 153632 | tf_op jit(solution)/shard_map/ppermute | solution.py:67
  225.6 1.0 fusion.11
  226.7 3.4 %collective-permute-done.29 = bf16[4,160,321]{2,1,0:T(8,128)(2,1)S(1)} collective-permute-done((bf16[4,160,321]{2,1,0:T(8,128)(2,1)S(1)}, bf16[4,160,321]{2,1,0:T(8,128)(2,1)S(1)}, u32[]{:S(2)}, u32[]{:S(2)}) %collective-permute-start.29) | collective-permute-done | bytes 410912 | tf_op jit(solution)/shard_map/ppermute | solution.py:57
  231.6 2.7 %collective-permute-start.31 = (bf16[160,321]{1,0:T(8,128)(2,1)S(1)}, bf16[160,321]{1,0:T(8,128)(2,1)}, u32[]{:S(2)}, u32[]{:S(2)}) collective-permute-start(bf16[160,321]{1,0:T(8,128)(2,1)S(1)} %get-tuple-element.48), channel_id=1, source_target_pairs={{0,16},{4,20},{8,24},{12,28},{16,0},{20,4},{24,8},{28,12},{1,17},{... | collective-permute-start | bytes 308168 | tf_op jit(solution)/shard_map/ppermute | solution.py:67
  234.3 1.3 collective-permute-start.32
  235.7 1.4 reshape.302
  237.1 2.2 collective-permute-done.30
  239.3 4.2 %collective-permute-done.31 = bf16[160,321]{1,0:T(8,128)(2,1)} collective-permute-done((bf16[160,321]{1,0:T(8,128)(2,1)S(1)}, bf16[160,321]{1,0:T(8,128)(2,1)}, u32[]{:S(2)}, u32[]{:S(2)}) %collective-permute-start.31) | collective-permute-done | bytes 102752 | tf_op jit(solution)/shard_map/ppermute | solution.py:67
  243.5 1.1 fusion.18
  (179 shorter events, 28.7 us)
Async XLA Ops:
  0.6 3.3 %copy-start = (bf16[384,2048]{1,0:T(8,128)(2,1)S(1)}, bf16[384,2048]{1,0:T(8,128)(2,1)}, u32[]{:S(2)}) copy-start(bf16[384,2048]{1,0:T(8,128)(2,1)} %param.11) | copy-start | bytes 4718596
  0.6 41.7 %collective-permute-start.2 = (bf16[320,384]{1,0:T(8,128)(2,1)}, bf16[320,384]{1,0:T(8,128)(2,1)}, u32[]{:S(2)}, u32[]{:S(2)}) collective-permute-start(bf16[320,384]{1,0:T(8,128)(2,1)} %bitcast.219), channel_id=1, source_target_pairs={{0,3},{1,0},{2,1},{3,2},{4,7},{5,4},{6,5},{7,6},{8,11},{9,8},{10,9... | collective-permute-start | bytes 737288 | tf_op jit(solution)/shard_map/ppermute | solution.py:180
  3.1 40.8 %collective-permute-start.3 = (bf16[320,384]{1,0:T(8,128)(2,1)}, bf16[320,384]{1,0:T(8,128)(2,1)}, u32[]{:S(2)}, u32[]{:S(2)}) collective-permute-start(bf16[320,384]{1,0:T(8,128)(2,1)} %bitcast.220), channel_id=1, source_target_pairs={{0,2},{1,3},{2,0},{3,1},{4,6},{5,7},{6,4},{7,5},{8,10},{9,11},{10,... | collective-permute-start | bytes 737288 | tf_op jit(solution)/shard_map/ppermute | solution.py:180
  3.8 41.2 %collective-permute-start.4 = (bf16[320,384]{1,0:T(8,128)(2,1)}, bf16[320,384]{1,0:T(8,128)(2,1)}, u32[]{:S(2)}, u32[]{:S(2)}) collective-permute-start(bf16[320,384]{1,0:T(8,128)(2,1)} %bitcast.221), channel_id=1, source_target_pairs={{0,1},{1,2},{2,3},{3,0},{4,5},{5,6},{6,7},{7,4},{8,9},{9,10},{10,1... | collective-permute-start | bytes 737288 | tf_op jit(solution)/shard_map/ppermute | solution.py:180
  3.9 8.6 %copy-start.26 = (s32[8,3]{0,1:T(4,128)S(1)}, s32[8,3]{0,1:T(4,128)}, u32[]{:S(2)}) copy-start(s32[8,3]{0,1:T(4,128)} %param.14) | copy-start | bytes 292
  3.9 8.9 %copy-start.21 = (bf16[384,1280]{1,0:T(8,128)(2,1)S(1)}, bf16[384,1280]{1,0:T(8,128)(2,1)}, u32[]{:S(2)}) copy-start(bf16[384,1280]{1,0:T(8,128)(2,1)} %param.12) | copy-start | bytes 2949124
  9.4 1.0 copy-start.18
  11.2 41.6 %collective-permute-start = (bf16[2,320,384]{2,1,0:T(8,128)(2,1)}, bf16[2,320,384]{2,1,0:T(8,128)(2,1)}, u32[]{:S(2)}, u32[]{:S(2)}) collective-permute-start(bf16[2,320,384]{2,1,0:T(8,128)(2,1)} %dynamic-slice_bitcast_fusion.1), channel_id=1, source_target_pairs={{0,1},{1,0},{2,3},{3,2},{4,5},{5,4},{6,7},{7,6},{8,9},{9,8},{10,11... | collective-permute-start | bytes 1474568 | tf_op jit(solution)/shard_map/ppermute | solution.py:57
  14.6 3.5 %copy-start.25 = (s32[8,3]{0,1:T(4,128)S(1)}, s32[8,3]{0,1:T(4,128)}, u32[]{:S(2)}) copy-start(s32[8,3]{0,1:T(4,128)} %param.15) | copy-start | bytes 292
  14.6 3.5 %copy-start.6 = (bf16[384,320]{0,1:T(8,128)(2,1)S(1)}, bf16[384,320]{0,1:T(8,128)(2,1)}, u32[]{:S(2)}) copy-start(bf16[384,320]{0,1:T(8,128)(2,1)} %param.13) | copy-start | bytes 737284
  16.6 52.7 %collective-permute-start.13 = (bf16[4,80,2048]{2,1,0:T(8,128)(2,1)}, bf16[4,80,2048]{2,1,0:T(8,128)(2,1)}, u32[]{:S(2)}, u32[]{:S(2)}) collective-permute-start(bf16[4,80,2048]{2,1,0:T(8,128)(2,1)} %bitcast.41), channel_id=1, source_target_pairs={{0,4},{4,0},{8,12},{12,8},{16,20},{20,16},{24,28},{28,24},{1,5},{5... | collective-permute-start | bytes 3932168 | tf_op jit(solution)/shard_map/ppermute | solution.py:57
  18.1 1.9 copy-start.31
  23.7 3.0 %copy-start.15 = (bf16[4,1,80,384]{3,2,1,0:T(8,128)(2,1)S(1)}, bf16[4,1,80,384]{3,2,1,0:T(8,128)(2,1)}, u32[]{:S(2)}) copy-start(bf16[4,1,80,384]{3,2,1,0:T(8,128)(2,1)} %get-tuple-element.56) | copy-start | bytes 737284
  26.7 1.9 copy-start.14
  28.6 7.1 %copy-start.24 = (f32[1280]{0:T(1024)S(1)}, f32[1280]{0:T(1024)}, u32[]{:S(2)}) copy-start(f32[1280]{0:T(1024)} %param.16) | copy-start | bytes 15364
  42.4 38.5 %collective-permute-start.17 = (bf16[4,80,2048]{2,1,0:T(8,128)(2,1)}, bf16[4,80,2048]{2,1,0:T(8,128)(2,1)}, u32[]{:S(2)}, u32[]{:S(2)}) collective-permute-start(bf16[4,80,2048]{2,1,0:T(8,128)(2,1)} %bitcast.51), channel_id=1, source_target_pairs={{0,4},{4,0},{8,12},{12,8},{16,20},{20,16},{24,28},{28,24},{1,5},{5... | collective-permute-start | bytes 3932168 | tf_op jit(solution)/shard_map/ppermute | solution.py:57
  49.0 1.7 copy-start.7
  50.7 2.1 copy-start.19
  54.0 8.2 %collective-permute-start.1 = (bf16[320,384]{1,0:T(8,128)(2,1)S(1)}, bf16[320,384]{1,0:T(8,128)(2,1)S(1)}, u32[]{:S(2)}, u32[]{:S(2)}) collective-permute-start(bf16[320,384]{1,0:T(8,128)(2,1)S(1)} %fusion.15), channel_id=1, source_target_pairs={{0,2},{1,3},{2,0},{3,1},{4,6},{5,7},{6,4},{7,5},{8,10},{9,11},{10,... | collective-permute-start | bytes 737288 | tf_op jit(solution)/shard_map/ppermute | solution.py:67
  55.6 6.7 %copy-start.28 = (pred[384]{0:T(512)(128)(4,1)S(1)}, pred[384]{0:T(512)(128)(4,1)}, u32[]{:S(2)}) copy-start(pred[384]{0:T(512)(128)(4,1)} %copy-done.27) | copy-start | bytes 1156
  55.6 6.8 %copy-start.29 = (pred[8]{0:T(512)(128)(4,1)S(1)}, pred[8]{0:T(512)(128)(4,1)}, u32[]{:S(2)}) copy-start(pred[8]{0:T(512)(128)(4,1)} %get-tuple-element.68) | copy-start | bytes 28
  55.6 6.8 %copy-start.30 = (pred[8]{0:T(512)(128)(4,1)S(1)}, pred[8]{0:T(512)(128)(4,1)}, u32[]{:S(2)}) copy-start(pred[8]{0:T(512)(128)(4,1)} %get-tuple-element.69) | copy-start | bytes 28
  62.2 7.1 %copy-start.4 = (bf16[320,2048]{1,0:T(8,128)(2,1)S(1)}, bf16[320,2048]{1,0:T(8,128)(2,1)}, u32[]{:S(2)}) copy-start(bf16[320,2048]{1,0:T(8,128)(2,1)} %convolution_convert_fusion.5) | copy-start | bytes 3932164
  63.5 73.7 %all-to-all-start = ((bf16[8,320,128]{2,1,0:T(8,128)(2,1)}), bf16[8,320,128]{2,1,0:T(8,128)(2,1)S(1)}, u32[]{:S(2)}, u32[]{:S(2)}) async-start(bf16[8,320,128]{2,1,0:T(8,128)(2,1)} %select_select_fusion), calls=%async_computation | async-start | bytes 1310720 | tf_op jit(solution)/shard_map/all_to_all | solution.py:224
  71.2 9.7 %copy-start.3 = (bf16[320,2048]{1,0:T(8,128)(2,1)S(1)}, bf16[320,2048]{1,0:T(8,128)(2,1)}, u32[]{:S(2)}) copy-start(bf16[320,2048]{1,0:T(8,128)(2,1)} %convolution_convert_fusion.3) | copy-start | bytes 3932164
  71.3 21.2 %collective-permute-start.14 = (bf16[80,2048]{1,0:T(8,128)(2,1)S(1)}, bf16[80,2048]{1,0:T(8,128)(2,1)S(1)}, u32[]{:S(2)}, u32[]{:S(2)}) collective-permute-start(bf16[80,2048]{1,0:T(8,128)(2,1)S(1)} %get-tuple-element.27), channel_id=1, source_target_pairs={{0,8},{4,12},{8,16},{12,20},{16,24},{20,28},{24,0},{28,4},{1,9},{5... | collective-permute-start | bytes 983048 | tf_op jit(solution)/shard_map/ppermute | solution.py:67
  73.4 49.6 %collective-permute-start.15 = (bf16[80,2048]{1,0:T(8,128)(2,1)S(1)}, bf16[80,2048]{1,0:T(8,128)(2,1)S(1)}, u32[]{:S(2)}, u32[]{:S(2)}) collective-permute-start(bf16[80,2048]{1,0:T(8,128)(2,1)S(1)} %get-tuple-element.29), channel_id=1, source_target_pairs={{0,16},{4,20},{8,24},{12,28},{16,0},{20,4},{24,8},{28,12},{1,17},{... | collective-permute-start | bytes 983048 | tf_op jit(solution)/shard_map/ppermute | solution.py:67
  75.7 47.2 %collective-permute-start.16 = (bf16[80,2048]{1,0:T(8,128)(2,1)S(1)}, bf16[80,2048]{1,0:T(8,128)(2,1)S(1)}, u32[]{:S(2)}, u32[]{:S(2)}) collective-permute-start(bf16[80,2048]{1,0:T(8,128)(2,1)S(1)} %get-tuple-element.28), channel_id=1, source_target_pairs={{0,24},{4,28},{8,0},{12,4},{16,8},{20,12},{24,16},{28,20},{1,25},{... | collective-permute-start | bytes 983048 | tf_op jit(solution)/shard_map/ppermute | solution.py:67
  82.9 40.3 %collective-permute-start.18 = (bf16[80,2048]{1,0:T(8,128)(2,1)S(1)}, bf16[80,2048]{1,0:T(8,128)(2,1)S(1)}, u32[]{:S(2)}, u32[]{:S(2)}) collective-permute-start(bf16[80,2048]{1,0:T(8,128)(2,1)S(1)} %get-tuple-element.30), channel_id=1, source_target_pairs={{0,8},{4,12},{8,16},{12,20},{16,24},{20,28},{24,0},{28,4},{1,9},{5... | collective-permute-start | bytes 983048 | tf_op jit(solution)/shard_map/ppermute | solution.py:67
  83.5 53.5 %collective-permute-start.19 = (bf16[80,2048]{1,0:T(8,128)(2,1)S(1)}, bf16[80,2048]{1,0:T(8,128)(2,1)S(1)}, u32[]{:S(2)}, u32[]{:S(2)}) collective-permute-start(bf16[80,2048]{1,0:T(8,128)(2,1)S(1)} %get-tuple-element.32), channel_id=1, source_target_pairs={{0,16},{4,20},{8,24},{12,28},{16,0},{20,4},{24,8},{28,12},{1,17},{... | collective-permute-start | bytes 983048 | tf_op jit(solution)/shard_map/ppermute | solution.py:67
  92.4 44.6 %collective-permute-start.20 = (bf16[80,2048]{1,0:T(8,128)(2,1)S(1)}, bf16[80,2048]{1,0:T(8,128)(2,1)S(1)}, u32[]{:S(2)}, u32[]{:S(2)}) collective-permute-start(bf16[80,2048]{1,0:T(8,128)(2,1)S(1)} %get-tuple-element.31), channel_id=1, source_target_pairs={{0,24},{4,28},{8,0},{12,4},{16,8},{20,12},{24,16},{28,20},{1,25},{... | collective-permute-start | bytes 983048 | tf_op jit(solution)/shard_map/ppermute | solution.py:67
  137.2 13.6 %copy-start.8 = (bf16[320,128]{1,0:T(8,128)(2,1)}, bf16[320,128]{1,0:T(8,128)(2,1)S(1)}, u32[]{:S(2)}) copy-start(bf16[320,128]{1,0:T(8,128)(2,1)S(1)} %get-tuple-element.43) | copy-start | bytes 245764
  137.2 13.6 %copy-start.10 = (bf16[320,128]{1,0:T(8,128)(2,1)}, bf16[320,128]{1,0:T(8,128)(2,1)S(1)}, u32[]{:S(2)}) copy-start(bf16[320,128]{1,0:T(8,128)(2,1)S(1)} %get-tuple-element.44) | copy-start | bytes 245764
  137.3 13.6 %copy-start.12 = (bf16[320,128]{1,0:T(8,128)(2,1)}, bf16[320,128]{1,0:T(8,128)(2,1)S(1)}, u32[]{:S(2)}) copy-start(bf16[320,128]{1,0:T(8,128)(2,1)S(1)} %get-tuple-element.45) | copy-start | bytes 245764
  137.3 4.3 %collective-permute-start.5 = (bf16[320,384]{1,0:T(8,128)(2,1)S(1)}, bf16[320,384]{1,0:T(8,128)(2,1)S(1)}, u32[]{:S(2)}, u32[]{:S(2)}) collective-permute-start(bf16[320,384]{1,0:T(8,128)(2,1)S(1)} %pad_maximum_fusion.2), channel_id=1, source_target_pairs={{0,3},{1,0},{2,1},{3,2},{4,7},{5,4},{6,5},{7,6},{8,11},{9,8},{10,9... | collective-permute-start | bytes 737288 | tf_op jit(solution)/shard_map/ppermute | solution.py:180
  138.5 11.0 %collective-permute-start.6 = (bf16[320,384]{1,0:T(8,128)(2,1)S(1)}, bf16[320,384]{1,0:T(8,128)(2,1)S(1)}, u32[]{:S(2)}, u32[]{:S(2)}) collective-permute-start(bf16[320,384]{1,0:T(8,128)(2,1)S(1)} %pad_maximum_fusion.2), channel_id=1, source_target_pairs={{0,2},{1,3},{2,0},{3,1},{4,6},{5,7},{6,4},{7,5},{8,10},{9,11},{10,... | collective-permute-start | bytes 737288 | tf_op jit(solution)/shard_map/ppermute | solution.py:180
  139.9 10.9 %collective-permute-start.7 = (bf16[320,384]{1,0:T(8,128)(2,1)S(1)}, bf16[320,384]{1,0:T(8,128)(2,1)S(1)}, u32[]{:S(2)}, u32[]{:S(2)}) collective-permute-start(bf16[320,384]{1,0:T(8,128)(2,1)S(1)} %pad_maximum_fusion.2), channel_id=1, source_target_pairs={{0,1},{1,2},{2,3},{3,0},{4,5},{5,6},{6,7},{7,4},{8,9},{9,10},{10,1... | collective-permute-start | bytes 737288 | tf_op jit(solution)/shard_map/ppermute | solution.py:180
  151.2 2.0 copy-start.5
  164.7 3.7 %copy-start.2 = (bf16[384,960]{1,0:T(8,128)(2,1)S(1)}, bf16[384,960]{1,0:T(8,128)(2,1)}, u32[]{:S(2)}) copy-start(bf16[384,960]{1,0:T(8,128)(2,1)} %get-tuple-element.12) | copy-start | bytes 2211844
  165.9 4.4 %copy-start.17 = (bf16[4,1,80,384]{3,2,1,0:T(8,128)(2,1)S(1)}, bf16[4,1,80,384]{3,2,1,0:T(8,128)(2,1)}, u32[]{:S(2)}) copy-start(bf16[4,1,80,384]{3,2,1,0:T(8,128)(2,1)} %get-tuple-element.71) | copy-start | bytes 737284
  165.9 5.5 %collective-permute-start.8 = (bf16[2,320,384]{2,1,0:T(8,128)(2,1)S(1)}, bf16[2,320,384]{2,1,0:T(8,128)(2,1)S(1)}, u32[]{:S(2)}, u32[]{:S(2)}) collective-permute-start(bf16[2,320,384]{2,1,0:T(8,128)(2,1)S(1)} %dynamic-slice_bitcast_fusion), channel_id=1, source_target_pairs={{0,1},{1,0},{2,3},{3,2},{4,5},{5,4},{6,7},{7,6},{8,9},{9,8},{10,11... | collective-permute-start | bytes 1474568 | tf_op jit(solution)/shard_map/ppermute | solution.py:57
  167.6 3.2 %copy-start.16 = (bf16[4,1,80,384]{3,2,1,0:T(8,128)(2,1)S(1)}, bf16[4,1,80,384]{3,2,1,0:T(8,128)(2,1)}, u32[]{:S(2)}) copy-start(bf16[4,1,80,384]{3,2,1,0:T(8,128)(2,1)} %get-tuple-element.51) | copy-start | bytes 737284
  167.6 17.7 %collective-permute-start.21 = (bf16[4,80,960]{2,1,0:T(8,128)(2,1)S(1)}, bf16[4,80,960]{2,1,0:T(8,128)(2,1)S(1)}, u32[]{:S(2)}, u32[]{:S(2)}) collective-permute-start(bf16[4,80,960]{2,1,0:T(8,128)(2,1)S(1)} %bitcast.244), channel_id=1, source_target_pairs={{0,4},{4,0},{8,12},{12,8},{16,20},{20,16},{24,28},{28,24},{1,5},{5... | collective-permute-start | bytes 1843208 | tf_op jit(solution)/shard_map/ppermute | solution.py:57
  169.0 2.4 copy-start.20
  169.0 29.9 %collective-permute-start.25 = (bf16[4,80,960]{2,1,0:T(8,128)(2,1)S(1)}, bf16[4,80,960]{2,1,0:T(8,128)(2,1)S(1)}, u32[]{:S(2)}, u32[]{:S(2)}) collective-permute-start(bf16[4,80,960]{2,1,0:T(8,128)(2,1)S(1)} %bitcast.243), channel_id=1, source_target_pairs={{0,4},{4,0},{8,12},{12,8},{16,20},{20,16},{24,28},{28,24},{1,5},{5... | collective-permute-start | bytes 1843208 | tf_op jit(solution)/shard_map/ppermute | solution.py:57
  171.5 28.7 %collective-permute-start.9 = (bf16[320,384]{1,0:T(8,128)(2,1)S(1)}, bf16[320,384]{1,0:T(8,128)(2,1)S(1)}, u32[]{:S(2)}, u32[]{:S(2)}) collective-permute-start(bf16[320,384]{1,0:T(8,128)(2,1)S(1)} %fusion.16), channel_id=1, source_target_pairs={{0,2},{1,3},{2,0},{3,1},{4,6},{5,7},{6,4},{7,5},{8,10},{9,11},{10,... | collective-permute-start | bytes 737288 | tf_op jit(solution)/shard_map/ppermute | solution.py:67
  187.5 27.7 %collective-permute-start.22 = (bf16[80,960]{1,0:T(8,128)(2,1)}, bf16[80,960]{1,0:T(8,128)(2,1)}, u32[]{:S(2)}, u32[]{:S(2)}) collective-permute-start(bf16[80,960]{1,0:T(8,128)(2,1)} %get-tuple-element.37), channel_id=1, source_target_pairs={{0,8},{4,12},{8,16},{12,20},{16,24},{20,28},{24,0},{28,4},{1,9},{5... | collective-permute-start | bytes 460808 | tf_op jit(solution)/shard_map/ppermute | solution.py:67
  193.2 23.0 %collective-permute-start.23 = (bf16[80,960]{1,0:T(8,128)(2,1)}, bf16[80,960]{1,0:T(8,128)(2,1)}, u32[]{:S(2)}, u32[]{:S(2)}) collective-permute-start(bf16[80,960]{1,0:T(8,128)(2,1)} %get-tuple-element.39), channel_id=1, source_target_pairs={{0,16},{4,20},{8,24},{12,28},{16,0},{20,4},{24,8},{28,12},{1,17},{... | collective-permute-start | bytes 460808 | tf_op jit(solution)/shard_map/ppermute | solution.py:67
  200.2 12.2 %copy-start.9 = (bf16[320,128]{1,0:T(8,128)(2,1)S(1)}, bf16[320,128]{1,0:T(8,128)(2,1)}, u32[]{:S(2)}) copy-start(bf16[320,128]{1,0:T(8,128)(2,1)} %copy-done.8) | copy-start | bytes 245764
  200.2 12.3 %copy-start.11 = (bf16[320,128]{1,0:T(8,128)(2,1)S(1)}, bf16[320,128]{1,0:T(8,128)(2,1)}, u32[]{:S(2)}) copy-start(bf16[320,128]{1,0:T(8,128)(2,1)} %copy-done.10) | copy-start | bytes 245764
  200.2 12.3 %copy-start.13 = (bf16[320,128]{1,0:T(8,128)(2,1)S(1)}, bf16[320,128]{1,0:T(8,128)(2,1)}, u32[]{:S(2)}) copy-start(bf16[320,128]{1,0:T(8,128)(2,1)} %copy-done.12) | copy-start | bytes 245764
  200.2 2.4 copy-start.22
  200.6 2.1 collective-permute-start.10
  200.6 8.8 %collective-permute-start.11 = (f32[1088]{0:T(1024)S(1)}, f32[1088]{0:T(1024)S(1)}, u32[]{:S(2)}, u32[]{:S(2)}) collective-permute-start(f32[1088]{0:T(1024)S(1)} %pad_maximum_fusion.3), channel_id=1, source_target_pairs={{0,2},{1,3},{2,0},{3,1},{4,6},{5,7},{6,4},{7,5},{8,10},{9,11},{10,... | collective-permute-start | bytes 13064 | tf_op jit(solution)/shard_map/ppermute | solution.py:180
  202.0 8.1 %collective-permute-start.12 = (f32[1088]{0:T(1024)S(1)}, f32[1088]{0:T(1024)S(1)}, u32[]{:S(2)}, u32[]{:S(2)}) collective-permute-start(f32[1088]{0:T(1024)S(1)} %pad_maximum_fusion.3), channel_id=1, source_target_pairs={{0,1},{1,2},{2,3},{3,0},{4,5},{5,6},{6,7},{7,4},{8,9},{9,10},{10,1... | collective-permute-start | bytes 13064 | tf_op jit(solution)/shard_map/ppermute | solution.py:180
  202.7 15.3 %collective-permute-start.24 = (bf16[80,960]{1,0:T(8,128)(2,1)}, bf16[80,960]{1,0:T(8,128)(2,1)S(1)}, u32[]{:S(2)}, u32[]{:S(2)}) collective-permute-start(bf16[80,960]{1,0:T(8,128)(2,1)} %get-tuple-element.38), channel_id=1, source_target_pairs={{0,24},{4,28},{8,0},{12,4},{16,8},{20,12},{24,16},{28,20},{1,25},{... | collective-permute-start | bytes 460808 | tf_op jit(solution)/shard_map/ppermute | solution.py:67
  209.4 9.8 %collective-permute-start.26 = (bf16[80,960]{1,0:T(8,128)(2,1)}, bf16[80,960]{1,0:T(8,128)(2,1)S(1)}, u32[]{:S(2)}, u32[]{:S(2)}) collective-permute-start(bf16[80,960]{1,0:T(8,128)(2,1)} %get-tuple-element.40), channel_id=1, source_target_pairs={{0,8},{4,12},{8,16},{12,20},{16,24},{20,28},{24,0},{28,4},{1,9},{5... | collective-permute-start | bytes 460808 | tf_op jit(solution)/shard_map/ppermute | solution.py:67
  210.1 15.6 %collective-permute-start.27 = (bf16[80,960]{1,0:T(8,128)(2,1)S(1)}, bf16[80,960]{1,0:T(8,128)(2,1)S(1)}, u32[]{:S(2)}, u32[]{:S(2)}) collective-permute-start(bf16[80,960]{1,0:T(8,128)(2,1)S(1)} %get-tuple-element.42), channel_id=1, source_target_pairs={{0,16},{4,20},{8,24},{12,28},{16,0},{20,4},{24,8},{28,12},{1,17},{... | collective-permute-start | bytes 460808 | tf_op jit(solution)/shard_map/ppermute | solution.py:67
  215.2 10.4 %collective-permute-start.28 = (bf16[80,960]{1,0:T(8,128)(2,1)S(1)}, bf16[80,960]{1,0:T(8,128)(2,1)S(1)}, u32[]{:S(2)}, u32[]{:S(2)}) collective-permute-start(bf16[80,960]{1,0:T(8,128)(2,1)S(1)} %get-tuple-element.41), channel_id=1, source_target_pairs={{0,24},{4,28},{8,0},{12,4},{16,8},{20,12},{24,16},{28,20},{1,25},{... | collective-permute-start | bytes 460808 | tf_op jit(solution)/shard_map/ppermute | solution.py:67
  216.2 13.8 %collective-permute-start.29 = (bf16[4,160,321]{2,1,0:T(8,128)(2,1)S(1)}, bf16[4,160,321]{2,1,0:T(8,128)(2,1)S(1)}, u32[]{:S(2)}, u32[]{:S(2)}) collective-permute-start(bf16[4,160,321]{2,1,0:T(8,128)(2,1)S(1)} %fusion.5), channel_id=1, source_target_pairs={{0,4},{4,0},{8,12},{12,8},{16,20},{20,16},{24,28},{28,24},{1,5},{5... | collective-permute-start | bytes 1232648 | tf_op jit(solution)/shard_map/ppermute | solution.py:57
  231.0 8.4 %collective-permute-start.30 = (bf16[160,321]{1,0:T(8,128)(2,1)}, bf16[160,321]{1,0:T(8,128)(2,1)}, u32[]{:S(2)}, u32[]{:S(2)}) collective-permute-start(bf16[160,321]{1,0:T(8,128)(2,1)} %get-tuple-element.46), channel_id=1, source_target_pairs={{0,8},{4,12},{8,16},{12,20},{16,24},{20,28},{24,0},{28,4},{1,9},{5... | collective-permute-start | bytes 308168 | tf_op jit(solution)/shard_map/ppermute | solution.py:67
  231.6 11.9 %collective-permute-start.31 = (bf16[160,321]{1,0:T(8,128)(2,1)S(1)}, bf16[160,321]{1,0:T(8,128)(2,1)}, u32[]{:S(2)}, u32[]{:S(2)}) collective-permute-start(bf16[160,321]{1,0:T(8,128)(2,1)S(1)} %get-tuple-element.48), channel_id=1, source_target_pairs={{0,16},{4,20},{8,24},{12,28},{16,0},{20,4},{24,8},{28,12},{1,17},{... | collective-permute-start | bytes 308168 | tf_op jit(solution)/shard_map/ppermute | solution.py:67
  234.3 11.7 %copy-start.1 = (bf16[384,2048]{1,0:T(8,128)(2,1)S(1)}, bf16[384,2048]{1,0:T(8,128)(2,1)}, u32[]{:S(2)}) copy-start(bf16[384,2048]{1,0:T(8,128)(2,1)} %param.11) | copy-start | bytes 4718596
  234.3 9.2 %collective-permute-start.32 = (bf16[160,321]{1,0:T(8,128)(2,1)S(1)}, bf16[160,321]{1,0:T(8,128)(2,1)}, u32[]{:S(2)}, u32[]{:S(2)}) collective-permute-start(bf16[160,321]{1,0:T(8,128)(2,1)S(1)} %get-tuple-element.47), channel_id=1, source_target_pairs={{0,24},{4,28},{8,0},{12,4},{16,8},{20,12},{24,16},{28,20},{1,25},{... | collective-permute-start | bytes 308168 | tf_op jit(solution)/shard_map/ppermute | solution.py:67
  (2 other events, 1.7 us)

commit v2 on v1

--- a/solution.py
+++ b/solution.py
@@ -255,11 +255,9 @@
         normed_in.reshape(groups, piece_rows, block_rows), packed_grad, "enc", inner, 2
     ).reshape(piece_rows, heads_here, 3 * head_size)
     out_term = jnp.dot(vis_low, mixed, preferred_element_type=jnp.float32).astype(jnp.bfloat16)
-    ln1_term = small[:, 2 * block_rows :].reshape(features_dim, 1).astype(jnp.bfloat16)
-    both = jnp.concatenate([out_term, ln1_term], axis=1)
-    both = two_stage_sum(both.reshape(groups, piece_rows, -1), None, "enc", inner)
-    grad_out = both[:, :-1].T
-    grad_ln1 = both[:, -1]
+    grad_out = two_stage_sum(out_term.reshape(groups, piece_rows, -1), None, "enc", inner).T
+    ln1_term = small[:, 2 * block_rows :].reshape(groups, piece_rows).astype(jnp.bfloat16)
+    grad_ln1 = two_stage_sum(ln1_term, None, "enc", inner)
     return (grad_input, grad_proj, grad_qkv, grad_out, grad_ln1)
 
 

time: 247 us -> 253 us (1.024)
  starting transfers between devices: 54.1 us -> 60 us
    ppermute x24 -> x28, starting transfers between devices: 41.9 us -> 47.8 us  [two_stage_sum(): arrived.append(lax.ppermute(sent, axis, pairs))]
    ppermute x24 -> x28, waiting for transfers between devices: 86.5 us -> 82.9 us  [two_stage_sum(): arrived.append(lax.ppermute(sent, axis, pairs))]
    unnamed x77 -> x68, local copies, waits for them, and re-layouts: 7.97 us -> 8.22 us
  transfers between devices with their start and end apart: 34 -> 38, of which waited for: 13 -> 18; matrix products, arithmetic and copies ran while one was open for 26% -> 26% of each run, Pallas kernels for 3% -> 3%
where the time goes in v2:
time: 253 us; the launch traced here: 251 us
  waiting for transfers between devices  95.7 us (38%)
  starting transfers between devices  60 us (24%)
  local copies, waits for them, and re-layouts  28.8 us (11%)
  other arithmetic  26.6 us (11%)
  matrix products  19 us (8%)
  Pallas kernels  18.3 us (7%)
  between operations  3.23 us (1%)
    ppermute x28, waiting for transfers between devices, two_stage_sum(): arrived.append(lax.ppermute(sent, axis, pairs))  82.9 us
    ppermute x28, starting transfers between devices, two_stage_sum(): arrived.append(lax.ppermute(sent, axis, pairs))  47.8 us
    ppermute x9, waiting for transfers between devices, gathered(): stacked.append(lax.ppermute(share, axis, pairs))  12.8 us
    pallas_call x1, Pallas kernels, attend_back(): pl.pallas_call(lambda *refs: attend_back_kernel(size, *refs), grid=(image...  11.7 us
    dot_general x8, matrix products, term(): jnp.dot(flat, right, preferred_element_type=jnp.float32)  10.8 us
    unnamed x68, local copies, waits for them, and re-layouts  8.22 us
    add x6, other arithmetic, two_stage_sum(): running += value.astype(jnp.float32)  7.69 us
    pallas_call x1, Pallas kernels, attend(): pl.pallas_call(lambda *refs: attend_kernel(size, *refs), grid=(images,),...  6.63 us
  transfers between devices with their start and end apart: 38, of which 18 were waited for; matrix products, arithmetic and copies ran while one was open for 26% of the time, Pallas kernels for 3%

profile of v2, /device:TPU:0, one launch (start us, length us, event | category | flops | bytes accessed | tf_op | source)
XLA Modules:
  0.0 251.5 jit_solution(3767312463022848742)
XLA Ops:
  0.6 2.5 collective-permute-start.2
  3.9 5.4 %convolution_convert_fusion = bf16[1280,384]{1,0:T(8,128)(2,1)S(1)} fusion(bf16[1280,2048]{1,0:T(8,128)(2,1)} %param.19, bf16[384,2048]{1,0:T(8,128)(2,1)S(1)} %copy-done), kind=kOutput, calls=%fused_computation.2 | convolution fusion | flops 2013757440 | bytes 7798784 | tf_op jit(solution)/shard_map/dot_general | solution.py:16
  11.1 1.4 collective-permute-start
  12.8 1.6 copy.46
  15.5 2.0 convolution_convert_fusion.4
  17.4 1.5 collective-permute-start.13
  19.6 1.4 reduce-window.8
  24.8 3.0 %convolution_convert_fusion.5 = bf16[320,2048]{1,0:T(8,128)(2,1)} fusion(bf16[320,384]{1,0:T(8,128)(2,1)} %bitcast.239, bf16[384,2048]{1,0:T(8,128)(2,1)S(1)} %copy-done), kind=kOutput, calls=%fused_computation.7 | convolution fusion | flops 503971840 | bytes 3129344 | tf_op jit(solution)/shard_map/dot_general | solution.py:50
  27.7 1.9 convolution_convert_fusion.2
  29.7 1.9 convolution_convert_fusion.3
  31.6 1.8 iota_compare_fusion.2
  34.9 1.4 fusion.18.refs_0_
  39.0 4.5 %copy.45.refs_4_ = bf16[1280,960]{1,0:T(8,128)(2,1)} copy(bf16[1280,960]{0,1:T(8,128)(2,1)} %bitcast.231) | data formatting | bytes 4915200 | tf_op jit(solution)/shard_map/reshape | solution.py:232
  50.6 1.2 copy-done.7
  51.9 2.1 convolution_convert_fusion.6.refs_1_.refs_0_
  54.0 1.1 convert_add_fusion.6
  56.9 6.6 %attend.1 = (f32[3,4,128,128]{3,2,1,0:T(8,128)}, bf16[384,320]{1,0:T(8,128)(2,1)}) custom-call(s32[3]{0:T(128)} %fusion.18.refs_0_, bf16[384,960]{1,0:T(8,128)(2,1)} %convolution_convert_fusion.6.refs_1_.refs_0_), custom_call_target="tpu_custom_call" | custom-call | flops 2000000000 | bytes 4000000 | tf_op jit(solution)/shard_map/attend/pallas_call | solution.py:105
  63.7 1.1 select_select_fusion
  64.8 5.8 %all-to-all-start = ((bf16[8,320,128]{2,1,0:T(8,128)(2,1)}), bf16[8,320,128]{2,1,0:T(8,128)(2,1)S(1)}, u32[]{:S(2)}, u32[]{:S(2)}) async-start(bf16[8,320,128]{2,1,0:T(8,128)(2,1)} %select_select_fusion), calls=%async_computation | async-start | bytes 1310720 | tf_op jit(solution)/shard_map/all_to_all | solution.py:224
  70.6 1.9 convert_add_fusion.1
  72.6 2.1 collective-permute-start.14
  74.7 2.4 collective-permute-start.15
  77.0 1.5 collective-permute-start.16
  78.5 3.1 %collective-permute-done.17 = bf16[4,80,2048]{2,1,0:T(8,128)(2,1)} collective-permute-done((bf16[4,80,2048]{2,1,0:T(8,128)(2,1)}, bf16[4,80,2048]{2,1,0:T(8,128)(2,1)}, u32[]{:S(2)}, u32[]{:S(2)}) %collective-permute-start.17) | collective-permute-done | bytes 1310752 | tf_op jit(solution)/shard_map/ppermute | solution.py:57
  81.6 1.9 convert_add_fusion
  84.4 4.5 %collective-permute-start.19 = (bf16[80,2048]{1,0:T(8,128)(2,1)S(1)}, bf16[80,2048]{1,0:T(8,128)(2,1)S(1)}, u32[]{:S(2)}, u32[]{:S(2)}) collective-permute-start(bf16[80,2048]{1,0:T(8,128)(2,1)S(1)} %get-tuple-element.37), channel_id=1, source_target_pairs={{0,16},{4,20},{8,24},{12,28},{16,0},{20,4},{24,8},{28,12},{1,17},{... | collective-permute-start | bytes 983048 | tf_op jit(solution)/shard_map/ppermute | solution.py:67
  88.8 4.9 %collective-permute-done.14 = bf16[80,2048]{1,0:T(8,128)(2,1)S(1)} collective-permute-done((bf16[80,2048]{1,0:T(8,128)(2,1)S(1)}, bf16[80,2048]{1,0:T(8,128)(2,1)S(1)}, u32[]{:S(2)}, u32[]{:S(2)}) %collective-permute-start.14) | collective-permute-done | bytes 327712 | tf_op jit(solution)/shard_map/ppermute | solution.py:67
  93.8 30.5 %collective-permute-done.15 = bf16[80,2048]{1,0:T(8,128)(2,1)S(1)} collective-permute-done((bf16[80,2048]{1,0:T(8,128)(2,1)S(1)}, bf16[80,2048]{1,0:T(8,128)(2,1)S(1)}, u32[]{:S(2)}, u32[]{:S(2)}) %collective-permute-start.15) | collective-permute-done | bytes 327712 | tf_op jit(solution)/shard_map/ppermute | solution.py:67
  124.4 13.9 %collective-permute-done.19 = bf16[80,2048]{1,0:T(8,128)(2,1)S(1)} collective-permute-done((bf16[80,2048]{1,0:T(8,128)(2,1)S(1)}, bf16[80,2048]{1,0:T(8,128)(2,1)S(1)}, u32[]{:S(2)}, u32[]{:S(2)}) %collective-permute-start.19) | collective-permute-done | bytes 327712 | tf_op jit(solution)/shard_map/ppermute | solution.py:67
  138.6 1.2 pad_maximum_fusion
  139.8 1.4 collective-permute-start.6
  141.5 1.4 collective-permute-done.5
  142.9 7.8 %collective-permute-done.6 = bf16[320,384]{1,0:T(8,128)(2,1)S(1)} collective-permute-done((bf16[320,384]{1,0:T(8,128)(2,1)S(1)}, bf16[320,384]{1,0:T(8,128)(2,1)S(1)}, u32[]{:S(2)}, u32[]{:S(2)}) %collective-permute-start.6) | collective-permute-done | bytes 245792 | tf_op jit(solution)/shard_map/ppermute | solution.py:180
  150.7 1.3 collective-permute-done.7
  153.3 11.7 %attend_back.1 = (bf16[384,960]{1,0:T(8,128)(2,1)}, bf16[1280,384]{1,0:T(8,128)(2,1)}) custom-call(bf16[384,960]{1,0:T(8,128)(2,1)} %convolution_convert_fusion.6.refs_1_.refs_0_, f32[3,4,128,128]{3,2,1,0:T(8,128)} %get-tuple-element.10.refs_1_, bf16[1280,384]{1,0:T(8,128)(2,1)} %bitcast.223, bf16[320,1280]{1,0:T(8,128)(2,1)} %refs_3_.1, ...), custom_call_target="tpu_custom_call" | custom-call | flops 3000000000 | bytes 6000000 | tf_op jit(solution)/shard_map/attend_back/pallas_call | solution.py:151
  165.0 1.9 dynamic-slice_bitcast_fusion.1
  169.6 1.3 collective-permute-start.21
  173.3 9.1 %collective-permute-done.29 = bf16[4,160,320]{2,1,0:T(8,128)(2,1)S(1)} collective-permute-done((bf16[4,160,320]{2,1,0:T(8,128)(2,1)S(1)}, bf16[4,160,320]{2,1,0:T(8,128)(2,1)S(1)}, u32[]{:S(2)}, u32[]{:S(2)}) %collective-permute-start.29) | collective-permute-done | bytes 409632 | tf_op jit(solution)/shard_map/ppermute | solution.py:57
  182.6 5.8 %collective-permute-start.30 = (bf16[160,320]{1,0:T(8,128)(2,1)S(1)}, bf16[160,320]{1,0:T(8,128)(2,1)S(1)}, u32[]{:S(2)}, u32[]{:S(2)}) collective-permute-start(bf16[160,320]{1,0:T(8,128)(2,1)S(1)} %get-tuple-element.51), channel_id=1, source_target_pairs={{0,8},{4,12},{8,16},{12,20},{16,24},{20,28},{24,0},{28,4},{1,9},{5... | collective-permute-start | bytes 307208 | tf_op jit(solution)/shard_map/ppermute | solution.py:67
  188.4 1.1 collective-permute-start.31
  189.5 1.3 collective-permute-start.32
  190.8 1.1 convert_add_fusion.5
  192.0 1.2 collective-permute-done.30
  193.2 1.3 collective-permute-start.9
  194.5 2.8 %collective-permute-done.31 = bf16[160,320]{1,0:T(8,128)(2,1)S(1)} collective-permute-done((bf16[160,320]{1,0:T(8,128)(2,1)S(1)}, bf16[160,320]{1,0:T(8,128)(2,1)S(1)}, u32[]{:S(2)}, u32[]{:S(2)}) %collective-permute-start.31) | collective-permute-done | bytes 102432 | tf_op jit(solution)/shard_map/ppermute | solution.py:67
  198.4 4.2 %collective-permute-start.22 = (bf16[80,960]{1,0:T(8,128)(2,1)S(1)}, bf16[80,960]{1,0:T(8,128)(2,1)}, u32[]{:S(2)}, u32[]{:S(2)}) collective-permute-start(bf16[80,960]{1,0:T(8,128)(2,1)S(1)} %get-tuple-element.42), channel_id=1, source_target_pairs={{0,8},{4,12},{8,16},{12,20},{16,24},{20,28},{24,0},{28,4},{1,9},{5... | collective-permute-start | bytes 460808 | tf_op jit(solution)/shard_map/ppermute | solution.py:67
  202.6 1.1 collective-permute-start.23
  203.7 6.4 %collective-permute-done.25 = bf16[4,80,960]{2,1,0:T(8,128)(2,1)S(1)} collective-permute-done((bf16[4,80,960]{2,1,0:T(8,128)(2,1)S(1)}, bf16[4,80,960]{2,1,0:T(8,128)(2,1)S(1)}, u32[]{:S(2)}, u32[]{:S(2)}) %collective-permute-start.25) | collective-permute-done | bytes 614432 | tf_op jit(solution)/shard_map/ppermute | solution.py:57
  210.0 1.4 convert_add_fusion.2
  211.8 1.3 collective-permute-start.11
  213.9 1.6 collective-permute-done.11
  216.7 1.3 concatenate.25
  220.6 1.6 fusion.10
  222.2 1.2 collective-permute-done.33
  223.4 5.8 %collective-permute-start.34 = (bf16[160]{0:T(256)(128)(2,1)S(1)}, bf16[160]{0:T(256)(128)(2,1)S(1)}, u32[]{:S(2)}, u32[]{:S(2)}) collective-permute-start(bf16[160]{0:T(256)(128)(2,1)S(1)} %get-tuple-element.17), channel_id=1, source_target_pairs={{0,8},{4,12},{8,16},{12,20},{16,24},{20,28},{24,0},{28,4},{1,9},{5... | collective-permute-start | bytes 968 | tf_op jit(solution)/shard_map/ppermute | solution.py:67
  229.2 1.6 collective-permute-start.35
  231.7 2.0 collective-permute-start.24
  234.3 1.4 collective-permute-start.27
  236.3 2.5 collective-permute-start.28
  238.7 4.7 %collective-permute-done.24 = bf16[80,960]{1,0:T(8,128)(2,1)S(1)} collective-permute-done((bf16[80,960]{1,0:T(8,128)(2,1)S(1)}, bf16[80,960]{1,0:T(8,128)(2,1)S(1)}, u32[]{:S(2)}, u32[]{:S(2)}) %collective-permute-start.24) | collective-permute-done | bytes 153632 | tf_op jit(solution)/shard_map/ppermute | solution.py:67
  243.4 1.1 fusion.9
  244.5 4.3 %collective-permute-done.27 = bf16[80,960]{1,0:T(8,128)(2,1)S(1)} collective-permute-done((bf16[80,960]{1,0:T(8,128)(2,1)}, bf16[80,960]{1,0:T(8,128)(2,1)S(1)}, u32[]{:S(2)}, u32[]{:S(2)}) %collective-permute-start.27) | collective-permute-done | bytes 153632 | tf_op jit(solution)/shard_map/ppermute | solution.py:67
  248.8 1.2 fusion.7
  250.1 1.4 reshape.291
  (181 shorter events, 36.0 us)
Async XLA Ops:
  0.6 3.3 %copy-start = (bf16[384,2048]{1,0:T(8,128)(2,1)S(1)}, bf16[384,2048]{1,0:T(8,128)(2,1)}, u32[]{:S(2)}) copy-start(bf16[384,2048]{1,0:T(8,128)(2,1)} %param.11) | copy-start | bytes 4718596
  0.6 42.9 %collective-permute-start.2 = (bf16[320,384]{1,0:T(8,128)(2,1)}, bf16[320,384]{1,0:T(8,128)(2,1)}, u32[]{:S(2)}, u32[]{:S(2)}) collective-permute-start(bf16[320,384]{1,0:T(8,128)(2,1)} %bitcast.226), channel_id=1, source_target_pairs={{0,3},{1,0},{2,1},{3,2},{4,7},{5,4},{6,5},{7,6},{8,11},{9,8},{10,9... | collective-permute-start | bytes 737288 | tf_op jit(solution)/shard_map/ppermute | solution.py:180
  3.1 42.0 %collective-permute-start.3 = (bf16[320,384]{1,0:T(8,128)(2,1)}, bf16[320,384]{1,0:T(8,128)(2,1)}, u32[]{:S(2)}, u32[]{:S(2)}) collective-permute-start(bf16[320,384]{1,0:T(8,128)(2,1)} %bitcast.227), channel_id=1, source_target_pairs={{0,2},{1,3},{2,0},{3,1},{4,6},{5,7},{6,4},{7,5},{8,10},{9,11},{10,... | collective-permute-start | bytes 737288 | tf_op jit(solution)/shard_map/ppermute | solution.py:180
  3.8 42.4 %collective-permute-start.4 = (bf16[320,384]{1,0:T(8,128)(2,1)}, bf16[320,384]{1,0:T(8,128)(2,1)}, u32[]{:S(2)}, u32[]{:S(2)}) collective-permute-start(bf16[320,384]{1,0:T(8,128)(2,1)} %bitcast.228), channel_id=1, source_target_pairs={{0,1},{1,2},{2,3},{3,0},{4,5},{5,6},{6,7},{7,4},{8,9},{9,10},{10,1... | collective-permute-start | bytes 737288 | tf_op jit(solution)/shard_map/ppermute | solution.py:180
  3.9 8.6 %copy-start.21 = (s32[8,3]{0,1:T(4,128)S(1)}, s32[8,3]{0,1:T(4,128)}, u32[]{:S(2)}) copy-start(s32[8,3]{0,1:T(4,128)} %param.14) | copy-start | bytes 292
  11.1 42.9 %collective-permute-start = (bf16[2,320,384]{2,1,0:T(8,128)(2,1)}, bf16[2,320,384]{2,1,0:T(8,128)(2,1)}, u32[]{:S(2)}, u32[]{:S(2)}) collective-permute-start(bf16[2,320,384]{2,1,0:T(8,128)(2,1)} %dynamic-slice_bitcast_fusion.2), channel_id=1, source_target_pairs={{0,1},{1,0},{2,3},{3,2},{4,5},{5,4},{6,7},{7,6},{8,9},{9,8},{10,11... | collective-permute-start | bytes 1474568 | tf_op jit(solution)/shard_map/ppermute | solution.py:57
  12.7 1.7 copy-start.22
  15.5 3.5 %copy-start.20 = (s32[8,3]{0,1:T(4,128)S(1)}, s32[8,3]{0,1:T(4,128)}, u32[]{:S(2)}) copy-start(s32[8,3]{0,1:T(4,128)} %param.15) | copy-start | bytes 292
  15.5 3.6 %copy-start.6 = (bf16[384,320]{0,1:T(8,128)(2,1)S(1)}, bf16[384,320]{0,1:T(8,128)(2,1)}, u32[]{:S(2)}) copy-start(bf16[384,320]{0,1:T(8,128)(2,1)} %param.13) | copy-start | bytes 737284
  17.4 53.2 %collective-permute-start.13 = (bf16[4,80,2048]{2,1,0:T(8,128)(2,1)}, bf16[4,80,2048]{2,1,0:T(8,128)(2,1)}, u32[]{:S(2)}, u32[]{:S(2)}) collective-permute-start(bf16[4,80,2048]{2,1,0:T(8,128)(2,1)} %bitcast.41), channel_id=1, source_target_pairs={{0,4},{4,0},{8,12},{12,8},{16,20},{20,16},{24,28},{28,24},{1,5},{5... | collective-permute-start | bytes 3932168 | tf_op jit(solution)/shard_map/ppermute | solution.py:57
  19.0 2.0 copy-start.26
  24.8 3.0 %copy-start.9 = (bf16[4,1,80,384]{3,2,1,0:T(8,128)(2,1)S(1)}, bf16[4,1,80,384]{3,2,1,0:T(8,128)(2,1)}, u32[]{:S(2)}) copy-start(bf16[4,1,80,384]{3,2,1,0:T(8,128)(2,1)} %get-tuple-element.61) | copy-start | bytes 737284
  27.7 2.0 copy-start.8
  29.7 7.2 %copy-start.18 = (f32[1280]{0:T(1024)S(1)}, f32[1280]{0:T(1024)}, u32[]{:S(2)}) copy-start(f32[1280]{0:T(1024)} %param.16) | copy-start | bytes 15364
  43.6 167.9 %copy-start.19 = (f32[320]{0:T(512)}, f32[320]{0:T(512)S(1)}, u32[]{:S(2)}) copy-start(f32[320]{0:T(512)S(1)} %dynamic_slice.190) | copy-start | bytes 3844
  43.6 38.1 %collective-permute-start.17 = (bf16[4,80,2048]{2,1,0:T(8,128)(2,1)}, bf16[4,80,2048]{2,1,0:T(8,128)(2,1)}, u32[]{:S(2)}, u32[]{:S(2)}) collective-permute-start(bf16[4,80,2048]{2,1,0:T(8,128)(2,1)} %bitcast.51), channel_id=1, source_target_pairs={{0,4},{4,0},{8,12},{12,8},{16,20},{20,16},{24,28},{28,24},{1,5},{5... | collective-permute-start | bytes 3932168 | tf_op jit(solution)/shard_map/ppermute | solution.py:57
  50.2 1.7 copy-start.7
  51.9 2.1 copy-start.15
  55.2 8.3 %collective-permute-start.1 = (bf16[320,384]{1,0:T(8,128)(2,1)S(1)}, bf16[320,384]{1,0:T(8,128)(2,1)S(1)}, u32[]{:S(2)}, u32[]{:S(2)}) collective-permute-start(bf16[320,384]{1,0:T(8,128)(2,1)S(1)} %fusion.11), channel_id=1, source_target_pairs={{0,2},{1,3},{2,0},{3,1},{4,6},{5,7},{6,4},{7,5},{8,10},{9,11},{10,... | collective-permute-start | bytes 737288 | tf_op jit(solution)/shard_map/ppermute | solution.py:67
  56.9 6.7 %copy-start.23 = (pred[384]{0:T(512)(128)(4,1)S(1)}, pred[384]{0:T(512)(128)(4,1)}, u32[]{:S(2)}) copy-start(pred[384]{0:T(512)(128)(4,1)} %copy-done.22) | copy-start | bytes 1156
  56.9 6.8 %copy-start.24 = (pred[8]{0:T(512)(128)(4,1)S(1)}, pred[8]{0:T(512)(128)(4,1)}, u32[]{:S(2)}) copy-start(pred[8]{0:T(512)(128)(4,1)} %get-tuple-element.75) | copy-start | bytes 28
  56.9 6.8 %copy-start.25 = (pred[8]{0:T(512)(128)(4,1)S(1)}, pred[8]{0:T(512)(128)(4,1)}, u32[]{:S(2)}) copy-start(pred[8]{0:T(512)(128)(4,1)} %get-tuple-element.76) | copy-start | bytes 28
  63.5 7.1 %copy-start.4 = (bf16[320,2048]{1,0:T(8,128)(2,1)S(1)}, bf16[320,2048]{1,0:T(8,128)(2,1)}, u32[]{:S(2)}) copy-start(bf16[320,2048]{1,0:T(8,128)(2,1)} %convolution_convert_fusion.5) | copy-start | bytes 3932164
  64.8 73.7 %all-to-all-start = ((bf16[8,320,128]{2,1,0:T(8,128)(2,1)}), bf16[8,320,128]{2,1,0:T(8,128)(2,1)S(1)}, u32[]{:S(2)}, u32[]{:S(2)}) async-start(bf16[8,320,128]{2,1,0:T(8,128)(2,1)} %select_select_fusion), calls=%async_computation | async-start | bytes 1310720 | tf_op jit(solution)/shard_map/all_to_all | solution.py:224
  72.5 9.2 %copy-start.3 = (bf16[320,2048]{1,0:T(8,128)(2,1)S(1)}, bf16[320,2048]{1,0:T(8,128)(2,1)}, u32[]{:S(2)}) copy-start(bf16[320,2048]{1,0:T(8,128)(2,1)} %convolution_convert_fusion.3) | copy-start | bytes 3932164
  72.6 21.2 %collective-permute-start.14 = (bf16[80,2048]{1,0:T(8,128)(2,1)S(1)}, bf16[80,2048]{1,0:T(8,128)(2,1)S(1)}, u32[]{:S(2)}, u32[]{:S(2)}) collective-permute-start(bf16[80,2048]{1,0:T(8,128)(2,1)S(1)} %get-tuple-element.32), channel_id=1, source_target_pairs={{0,8},{4,12},{8,16},{12,20},{16,24},{20,28},{24,0},{28,4},{1,9},{5... | collective-permute-start | bytes 983048 | tf_op jit(solution)/shard_map/ppermute | solution.py:67
  74.7 49.6 %collective-permute-start.15 = (bf16[80,2048]{1,0:T(8,128)(2,1)S(1)}, bf16[80,2048]{1,0:T(8,128)(2,1)S(1)}, u32[]{:S(2)}, u32[]{:S(2)}) collective-permute-start(bf16[80,2048]{1,0:T(8,128)(2,1)S(1)} %get-tuple-element.34), channel_id=1, source_target_pairs={{0,16},{4,20},{8,24},{12,28},{16,0},{20,4},{24,8},{28,12},{1,17},{... | collective-permute-start | bytes 983048 | tf_op jit(solution)/shard_map/ppermute | solution.py:67
  77.0 47.2 %collective-permute-start.16 = (bf16[80,2048]{1,0:T(8,128)(2,1)S(1)}, bf16[80,2048]{1,0:T(8,128)(2,1)S(1)}, u32[]{:S(2)}, u32[]{:S(2)}) collective-permute-start(bf16[80,2048]{1,0:T(8,128)(2,1)S(1)} %get-tuple-element.33), channel_id=1, source_target_pairs={{0,24},{4,28},{8,0},{12,4},{16,8},{20,12},{24,16},{28,20},{1,25},{... | collective-permute-start | bytes 983048 | tf_op jit(solution)/shard_map/ppermute | solution.py:67
  83.6 40.8 %collective-permute-start.18 = (bf16[80,2048]{1,0:T(8,128)(2,1)S(1)}, bf16[80,2048]{1,0:T(8,128)(2,1)S(1)}, u32[]{:S(2)}, u32[]{:S(2)}) collective-permute-start(bf16[80,2048]{1,0:T(8,128)(2,1)S(1)} %get-tuple-element.35), channel_id=1, source_target_pairs={{0,8},{4,12},{8,16},{12,20},{16,24},{20,28},{24,0},{28,4},{1,9},{5... | collective-permute-start | bytes 983048 | tf_op jit(solution)/shard_map/ppermute | solution.py:67
  84.4 53.9 %collective-permute-start.19 = (bf16[80,2048]{1,0:T(8,128)(2,1)S(1)}, bf16[80,2048]{1,0:T(8,128)(2,1)S(1)}, u32[]{:S(2)}, u32[]{:S(2)}) collective-permute-start(bf16[80,2048]{1,0:T(8,128)(2,1)S(1)} %get-tuple-element.37), channel_id=1, source_target_pairs={{0,16},{4,20},{8,24},{12,28},{16,0},{20,4},{24,8},{28,12},{1,17},{... | collective-permute-start | bytes 983048 | tf_op jit(solution)/shard_map/ppermute | solution.py:67
  93.7 44.6 %collective-permute-start.20 = (bf16[80,2048]{1,0:T(8,128)(2,1)S(1)}, bf16[80,2048]{1,0:T(8,128)(2,1)S(1)}, u32[]{:S(2)}, u32[]{:S(2)}) collective-permute-start(bf16[80,2048]{1,0:T(8,128)(2,1)S(1)} %get-tuple-element.36), channel_id=1, source_target_pairs={{0,24},{4,28},{8,0},{12,4},{16,8},{20,12},{24,16},{28,20},{1,25},{... | collective-permute-start | bytes 983048 | tf_op jit(solution)/shard_map/ppermute | solution.py:67
  138.6 4.3 %collective-permute-start.5 = (bf16[320,384]{1,0:T(8,128)(2,1)S(1)}, bf16[320,384]{1,0:T(8,128)(2,1)S(1)}, u32[]{:S(2)}, u32[]{:S(2)}) collective-permute-start(bf16[320,384]{1,0:T(8,128)(2,1)S(1)} %pad_maximum_fusion.2), channel_id=1, source_target_pairs={{0,3},{1,0},{2,1},{3,2},{4,7},{5,4},{6,5},{7,6},{8,11},{9,8},{10,9... | collective-permute-start | bytes 737288 | tf_op jit(solution)/shard_map/ppermute | solution.py:180
  139.8 10.9 %collective-permute-start.6 = (bf16[320,384]{1,0:T(8,128)(2,1)S(1)}, bf16[320,384]{1,0:T(8,128)(2,1)S(1)}, u32[]{:S(2)}, u32[]{:S(2)}) collective-permute-start(bf16[320,384]{1,0:T(8,128)(2,1)S(1)} %pad_maximum_fusion.2), channel_id=1, source_target_pairs={{0,2},{1,3},{2,0},{3,1},{4,6},{5,7},{6,4},{7,5},{8,10},{9,11},{10,... | collective-permute-start | bytes 737288 | tf_op jit(solution)/shard_map/ppermute | solution.py:180
  141.2 10.8 %collective-permute-start.7 = (bf16[320,384]{1,0:T(8,128)(2,1)S(1)}, bf16[320,384]{1,0:T(8,128)(2,1)S(1)}, u32[]{:S(2)}, u32[]{:S(2)}) collective-permute-start(bf16[320,384]{1,0:T(8,128)(2,1)S(1)} %pad_maximum_fusion.2), channel_id=1, source_target_pairs={{0,1},{1,2},{2,3},{3,0},{4,5},{5,6},{6,7},{7,4},{8,9},{9,10},{10,1... | collective-permute-start | bytes 737288 | tf_op jit(solution)/shard_map/ppermute | solution.py:180
  153.3 13.5 %copy-start.5 = (bf16[4,320,384]{2,1,0:T(8,128)(2,1)S(1)}, bf16[4,320,384]{2,1,0:T(8,128)(2,1)}, u32[]{:S(2)}) copy-start(bf16[4,320,384]{2,1,0:T(8,128)(2,1)} %constant_dynamic-slice_fusion.15) | copy-start | bytes 2949124
  153.3 13.5 %copy-start.17 = (bf16[384,320]{1,0:T(8,128)(2,1)S(1)}, bf16[384,320]{1,0:T(8,128)(2,1)}, u32[]{:S(2)}) copy-start(bf16[384,320]{1,0:T(8,128)(2,1)} %get-tuple-element.13) | copy-start | bytes 737284
  166.9 22.6 %collective-permute-start.8 = (bf16[2,320,384]{2,1,0:T(8,128)(2,1)}, bf16[2,320,384]{2,1,0:T(8,128)(2,1)}, u32[]{:S(2)}, u32[]{:S(2)}) collective-permute-start(bf16[2,320,384]{2,1,0:T(8,128)(2,1)} %dynamic-slice_bitcast_fusion.1), channel_id=1, source_target_pairs={{0,1},{1,0},{2,3},{3,2},{4,5},{5,4},{6,7},{7,6},{8,9},{9,8},{10,11... | collective-permute-start | bytes 1474568 | tf_op jit(solution)/shard_map/ppermute | solution.py:57
  167.5 1.6 copy-start.2
  167.5 1.6 copy-start.13
  168.2 2.8 %copy-start.12 = (bf16[4,1,80,384]{3,2,1,0:T(8,128)(2,1)S(1)}, bf16[4,1,80,384]{3,2,1,0:T(8,128)(2,1)}, u32[]{:S(2)}) copy-start(bf16[4,1,80,384]{3,2,1,0:T(8,128)(2,1)} %get-tuple-element.57) | copy-start | bytes 737284
  168.2 4.0 %copy-start.11 = (bf16[4,1,80,384]{3,2,1,0:T(8,128)(2,1)S(1)}, bf16[4,1,80,384]{3,2,1,0:T(8,128)(2,1)}, u32[]{:S(2)}) copy-start(bf16[4,1,80,384]{3,2,1,0:T(8,128)(2,1)} %get-tuple-element.78) | copy-start | bytes 737284
  168.3 14.2 %collective-permute-start.29 = (bf16[4,160,320]{2,1,0:T(8,128)(2,1)S(1)}, bf16[4,160,320]{2,1,0:T(8,128)(2,1)S(1)}, u32[]{:S(2)}, u32[]{:S(2)}) collective-permute-start(bf16[4,160,320]{2,1,0:T(8,128)(2,1)S(1)} %dynamic-slice_bitcast_fusion), channel_id=1, source_target_pairs={{0,4},{4,0},{8,12},{12,8},{16,20},{20,16},{24,28},{28,24},{1,5},{5... | collective-permute-start | bytes 1228808 | tf_op jit(solution)/shard_map/ppermute | solution.py:57
  169.6 3.2 %copy-start.10 = (bf16[4,1,80,384]{3,2,1,0:T(8,128)(2,1)S(1)}, bf16[4,1,80,384]{3,2,1,0:T(8,128)(2,1)}, u32[]{:S(2)}) copy-start(bf16[4,1,80,384]{3,2,1,0:T(8,128)(2,1)} %get-tuple-element.56) | copy-start | bytes 737284
  169.6 28.4 %collective-permute-start.21 = (bf16[4,80,960]{2,1,0:T(8,128)(2,1)S(1)}, bf16[4,80,960]{2,1,0:T(8,128)(2,1)S(1)}, u32[]{:S(2)}, u32[]{:S(2)}) collective-permute-start(bf16[4,80,960]{2,1,0:T(8,128)(2,1)S(1)} %bitcast.251), channel_id=1, source_target_pairs={{0,4},{4,0},{8,12},{12,8},{16,20},{20,16},{24,28},{28,24},{1,5},{5... | collective-permute-start | bytes 1843208 | tf_op jit(solution)/shard_map/ppermute | solution.py:57
  171.5 38.6 %collective-permute-start.25 = (bf16[4,80,960]{2,1,0:T(8,128)(2,1)S(1)}, bf16[4,80,960]{2,1,0:T(8,128)(2,1)S(1)}, u32[]{:S(2)}, u32[]{:S(2)}) collective-permute-start(bf16[4,80,960]{2,1,0:T(8,128)(2,1)S(1)} %bitcast.250), channel_id=1, source_target_pairs={{0,4},{4,0},{8,12},{12,8},{16,20},{20,16},{24,28},{28,24},{1,5},{5... | collective-permute-start | bytes 1843208 | tf_op jit(solution)/shard_map/ppermute | solution.py:57
  173.3 17.5 %copy-start.16 = (bf16[1280,384]{1,0:T(8,128)(2,1)S(1)}, bf16[1280,384]{1,0:T(8,128)(2,1)}, u32[]{:S(2)}) copy-start(bf16[1280,384]{1,0:T(8,128)(2,1)} %get-tuple-element.11) | copy-start | bytes 2949124
  182.6 10.6 %collective-permute-start.30 = (bf16[160,320]{1,0:T(8,128)(2,1)S(1)}, bf16[160,320]{1,0:T(8,128)(2,1)S(1)}, u32[]{:S(2)}, u32[]{:S(2)}) collective-permute-start(bf16[160,320]{1,0:T(8,128)(2,1)S(1)} %get-tuple-element.51), channel_id=1, source_target_pairs={{0,8},{4,12},{8,16},{12,20},{16,24},{20,28},{24,0},{28,4},{1,9},{5... | collective-permute-start | bytes 307208 | tf_op jit(solution)/shard_map/ppermute | solution.py:67
  188.4 8.9 %collective-permute-start.31 = (bf16[160,320]{1,0:T(8,128)(2,1)S(1)}, bf16[160,320]{1,0:T(8,128)(2,1)S(1)}, u32[]{:S(2)}, u32[]{:S(2)}) collective-permute-start(bf16[160,320]{1,0:T(8,128)(2,1)S(1)} %get-tuple-element.53), channel_id=1, source_target_pairs={{0,16},{4,20},{8,24},{12,28},{16,0},{20,4},{24,8},{28,12},{1,17},{... | collective-permute-start | bytes 307208 | tf_op jit(solution)/shard_map/ppermute | solution.py:67
  189.5 7.8 %collective-permute-start.32 = (bf16[160,320]{1,0:T(8,128)(2,1)S(1)}, bf16[160,320]{1,0:T(8,128)(2,1)S(1)}, u32[]{:S(2)}, u32[]{:S(2)}) collective-permute-start(bf16[160,320]{1,0:T(8,128)(2,1)S(1)} %get-tuple-element.52), channel_id=1, source_target_pairs={{0,24},{4,28},{8,0},{12,4},{16,8},{20,12},{24,16},{28,20},{1,25},{... | collective-permute-start | bytes 307208 | tf_op jit(solution)/shard_map/ppermute | solution.py:67
  193.2 18.3 %collective-permute-start.9 = (bf16[320,384]{1,0:T(8,128)(2,1)S(1)}, bf16[320,384]{1,0:T(8,128)(2,1)S(1)}, u32[]{:S(2)}, u32[]{:S(2)}) collective-permute-start(bf16[320,384]{1,0:T(8,128)(2,1)S(1)} %fusion.12), channel_id=1, source_target_pairs={{0,2},{1,3},{2,0},{3,1},{4,6},{5,7},{6,4},{7,5},{8,10},{9,11},{10,... | collective-permute-start | bytes 737288 | tf_op jit(solution)/shard_map/ppermute | solution.py:67
  198.4 37.9 %collective-permute-start.22 = (bf16[80,960]{1,0:T(8,128)(2,1)S(1)}, bf16[80,960]{1,0:T(8,128)(2,1)}, u32[]{:S(2)}, u32[]{:S(2)}) collective-permute-start(bf16[80,960]{1,0:T(8,128)(2,1)S(1)} %get-tuple-element.42), channel_id=1, source_target_pairs={{0,8},{4,12},{8,16},{12,20},{16,24},{20,28},{24,0},{28,4},{1,9},{5... | collective-permute-start | bytes 460808 | tf_op jit(solution)/shard_map/ppermute | solution.py:67
  202.6 36.2 %collective-permute-start.23 = (bf16[80,960]{1,0:T(8,128)(2,1)S(1)}, bf16[80,960]{1,0:T(8,128)(2,1)}, u32[]{:S(2)}, u32[]{:S(2)}) collective-permute-start(bf16[80,960]{1,0:T(8,128)(2,1)S(1)} %get-tuple-element.44), channel_id=1, source_target_pairs={{0,16},{4,20},{8,24},{12,28},{16,0},{20,4},{24,8},{28,12},{1,17},{... | collective-permute-start | bytes 460808 | tf_op jit(solution)/shard_map/ppermute | solution.py:67
  211.7 2.1 collective-permute-start.10
  211.8 3.7 %collective-permute-start.11 = (f32[1088]{0:T(1024)S(1)}, f32[1088]{0:T(1024)S(1)}, u32[]{:S(2)}, u32[]{:S(2)}) collective-permute-start(f32[1088]{0:T(1024)S(1)} %pad_maximum_fusion.3), channel_id=1, source_target_pairs={{0,2},{1,3},{2,0},{3,1},{4,6},{5,7},{6,4},{7,5},{8,10},{9,11},{10,... | collective-permute-start | bytes 13064 | tf_op jit(solution)/shard_map/ppermute | solution.py:180
  213.1 3.1 %collective-permute-start.12 = (f32[1088]{0:T(1024)S(1)}, f32[1088]{0:T(1024)S(1)}, u32[]{:S(2)}, u32[]{:S(2)}) collective-permute-start(f32[1088]{0:T(1024)S(1)} %pad_maximum_fusion.3), channel_id=1, source_target_pairs={{0,1},{1,2},{2,3},{3,0},{4,5},{5,6},{6,7},{7,4},{8,9},{9,10},{10,1... | collective-permute-start | bytes 13064 | tf_op jit(solution)/shard_map/ppermute | solution.py:180
  219.8 3.7 %collective-permute-start.33 = (bf16[4,160]{1,0:T(4,128)(2,1)S(1)}, bf16[4,160]{1,0:T(4,128)(2,1)S(1)}, u32[]{:S(2)}, u32[]{:S(2)}) collective-permute-start(bf16[4,160]{1,0:T(4,128)(2,1)S(1)} %bitcast.253), channel_id=1, source_target_pairs={{0,4},{4,0},{8,12},{12,8},{16,20},{20,16},{24,28},{28,24},{1,5},{5... | collective-permute-start | bytes 3848 | tf_op jit(solution)/shard_map/ppermute | solution.py:57
  223.4 8.3 %collective-permute-start.34 = (bf16[160]{0:T(256)(128)(2,1)S(1)}, bf16[160]{0:T(256)(128)(2,1)S(1)}, u32[]{:S(2)}, u32[]{:S(2)}) collective-permute-start(bf16[160]{0:T(256)(128)(2,1)S(1)} %get-tuple-element.17), channel_id=1, source_target_pairs={{0,8},{4,12},{8,16},{12,20},{16,24},{20,28},{24,0},{28,4},{1,9},{5... | collective-permute-start | bytes 968 | tf_op jit(solution)/shard_map/ppermute | solution.py:67
  229.2 4.6 %collective-permute-start.35 = (bf16[160]{0:T(256)(128)(2,1)S(1)}, bf16[160]{0:T(256)(128)(2,1)S(1)}, u32[]{:S(2)}, u32[]{:S(2)}) collective-permute-start(bf16[160]{0:T(256)(128)(2,1)S(1)} %get-tuple-element.19), channel_id=1, source_target_pairs={{0,16},{4,20},{8,24},{12,28},{16,0},{20,4},{24,8},{28,12},{1,17},{... | collective-permute-start | bytes 968 | tf_op jit(solution)/shard_map/ppermute | solution.py:67
  230.7 3.6 %collective-permute-start.36 = (bf16[160]{0:T(256)(128)(2,1)S(1)}, bf16[160]{0:T(256)(128)(2,1)S(1)}, u32[]{:S(2)}, u32[]{:S(2)}) collective-permute-start(bf16[160]{0:T(256)(128)(2,1)S(1)} %get-tuple-element.18), channel_id=1, source_target_pairs={{0,24},{4,28},{8,0},{12,4},{16,8},{20,12},{24,16},{28,20},{1,25},{... | collective-permute-start | bytes 968 | tf_op jit(solution)/shard_map/ppermute | solution.py:67
  231.7 11.7 %collective-permute-start.24 = (bf16[80,960]{1,0:T(8,128)(2,1)S(1)}, bf16[80,960]{1,0:T(8,128)(2,1)S(1)}, u32[]{:S(2)}, u32[]{:S(2)}) collective-permute-start(bf16[80,960]{1,0:T(8,128)(2,1)S(1)} %get-tuple-element.43), channel_id=1, source_target_pairs={{0,24},{4,28},{8,0},{12,4},{16,8},{20,12},{24,16},{28,20},{1,25},{... | collective-permute-start | bytes 460808 | tf_op jit(solution)/shard_map/ppermute | solution.py:67
  233.8 10.8 %collective-permute-start.26 = (bf16[80,960]{1,0:T(8,128)(2,1)}, bf16[80,960]{1,0:T(8,128)(2,1)S(1)}, u32[]{:S(2)}, u32[]{:S(2)}) collective-permute-start(bf16[80,960]{1,0:T(8,128)(2,1)} %get-tuple-element.45), channel_id=1, source_target_pairs={{0,8},{4,12},{8,16},{12,20},{16,24},{20,28},{24,0},{28,4},{1,9},{5... | collective-permute-start | bytes 460808 | tf_op jit(solution)/shard_map/ppermute | solution.py:67
  234.3 14.5 %collective-permute-start.27 = (bf16[80,960]{1,0:T(8,128)(2,1)}, bf16[80,960]{1,0:T(8,128)(2,1)S(1)}, u32[]{:S(2)}, u32[]{:S(2)}) collective-permute-start(bf16[80,960]{1,0:T(8,128)(2,1)} %get-tuple-element.47), channel_id=1, source_target_pairs={{0,16},{4,20},{8,24},{12,28},{16,0},{20,4},{24,8},{28,12},{1,17},{... | collective-permute-start | bytes 460808 | tf_op jit(solution)/shard_map/ppermute | solution.py:67
  236.3 12.6 %collective-permute-start.28 = (bf16[80,960]{1,0:T(8,128)(2,1)}, bf16[80,960]{1,0:T(8,128)(2,1)S(1)}, u32[]{:S(2)}, u32[]{:S(2)}) collective-permute-start(bf16[80,960]{1,0:T(8,128)(2,1)} %get-tuple-element.46), channel_id=1, source_target_pairs={{0,24},{4,28},{8,0},{12,4},{16,8},{20,12},{24,16},{28,20},{1,25},{... | collective-permute-start | bytes 460808 | tf_op jit(solution)/shard_map/ppermute | solution.py:67
  248.8 2.6 %copy-start.1 = (bf16[384,2048]{1,0:T(8,128)(2,1)S(1)}, bf16[384,2048]{1,0:T(8,128)(2,1)}, u32[]{:S(2)}) copy-start(bf16[384,2048]{1,0:T(8,128)(2,1)} %param.11) | copy-start | bytes 4718596
  (1 other events, 1.0 us)
